TPU v7x, 32 devices: a whole 2x2x4 slice. The times are simulated.
32 devices in a mesh: ctx: 8 (over y, x, core), head: 4 (over z).
Axes of the slice: x: 2, y: 2, z: 4, core: 2. Of those that a mesh axis runs over, the one named last changes fastest.
Arguments:
- tokens: bfloat16 [2, 2048, 2048], P(None, 'ctx'), may hold values from -6 to 6
- w_qkv: bfloat16 [2048, 4, 1536], P(None, 'head'), as said below
- w_rate: bfloat16 [2048, 4], P(None, 'head'), may hold values from -0.125 to 0.125
- w_out: bfloat16 [4, 512, 2048], P('head'), may hold values from -0.125 to 0.125
- fw_gain: float32 [4, 512], P('head'), may hold values from 0.25 to 1.75
- fast_first: float32 [4, 512, 512], P('head'), may hold values from -0.25 to 0.25
- fast_third: float32 [4, 512, 512], P('head'), may hold values from -0.25 to 0.25
- fast_second: float32 [4, 512, 512], P('head'), may hold values from -0.25 to 0.25
Outputs:
- mixed: bfloat16 [2, 2048, 2048], P(None, 'ctx', 'head')
- new_first: float32 [4, 512, 512], P('head')
- new_third: float32 [4, 512, 512], P('head')
- new_second: float32 [4, 512, 512], P('head')
Inputs may be any that keep to these rules, and one draw needn't show every extreme that they name: `w_qkv`: A projection scaled by its fan-in 2048.
All inputs are finite; a program needn't handle non-finite values.
Results may differ from a plain program's by a relative error of at most 0.039.
Values may be sent and summed in bfloat16 or wider, within the bound.
A program may use at most 128 MiB of HBM per device.

v0:
```python
import functools

import jax
import jax.numpy as jnp
from jax import lax
from jax.experimental import pallas as pl
from jax.experimental.pallas import tpu as pltpu
from jax.sharding import PartitionSpec as P

WINDOW = 2048
NS_STEPS = 5

coeff_a = 3.4445
coeff_b = -4.775
coeff_c = 2.0315
fast_step = 0.5
norm_eps = 1e-06
BF = jnp.bfloat16
F32 = jnp.float32
VMEM = pl.BlockSpec(memory_space=pltpu.VMEM)
LIMIT = 60 * 1024 * 1024


def mm(left, right, dims):
    return lax.dot_general(left, right, (dims, ((), ())), preferred_element_type=F32)


def nn(left, right):
    return mm(left, right, ((1,), (0,)))


def nt(left, right):
    return mm(left, right, ((1,), (1,)))


def tn(left, right):
    return mm(left, right, ((0,), (0,)))


def project_kernel(rows, tok, w, wr, f1, f3, f2, q_ref, kv_ref, g_ref, kv_s):
    step = pl.program_id(0)
    res = nn(tok[...], w[...]).astype(BF)

    @pl.when(step < 2)
    def _():
        kv_ref[...] = res
        kv_s[step] = res

    @pl.when(step == 2)
    def _():
        q_ref[...] = res
        keys = kv_s[0, :rows]
        vals = kv_s[1, :rows]
        logit = jnp.sum(
            tok[:rows].astype(F32) * wr[...].astype(F32), axis=1, keepdims=True
        )
        rate = jnp.maximum(logit, 0.0) + jnp.log1p(jnp.exp(-jnp.abs(logit)))
        target = (-rate * vals.astype(F32)).astype(BF)
        h1 = nn(keys, f1[...].astype(BF))
        h3 = nn(keys, f3[...].astype(BF))
        sig = jax.nn.sigmoid(h1)
        silu = h1 * sig
        act = (silu * h3).astype(BF)
        dact = nt(target, f2[...].astype(BF))
        d1 = (dact * h3 * (sig * (1.0 + h1 * (1.0 - sig)))).astype(BF)
        d3 = (dact * silu).astype(BF)
        g_ref[0] = tn(keys, d1).astype(BF)
        g_ref[1] = tn(keys, d3).astype(BF)
        g_ref[2] = tn(act, target).astype(BF)


def project(flat, rows, w_qkv, w_rate, f1, f3, f2):
    total, width = flat.shape
    dh = f1.shape[0]
    fh = f1.shape[1]
    whole = lambda *shape: pl.BlockSpec(shape, lambda n: (0,) * len(shape))
    return pl.pallas_call(
        functools.partial(project_kernel, rows),
        grid=(3,),
        in_specs=[
            whole(total, width),
            pl.BlockSpec((width, dh), lambda n: (0, lax.rem(n + 1, 3))),
            whole(1, width),
            whole(dh, fh),
            whole(dh, fh),
            whole(fh, dh),
        ],
        out_specs=[
            whole(total, dh),
            pl.BlockSpec((total, dh), lambda n: (0, jnp.minimum(n, 1))),
            whole(3, dh, fh),
        ],
        out_shape=[
            jax.ShapeDtypeStruct((total, dh), BF),
            jax.ShapeDtypeStruct((total, 2 * dh), BF),
            jax.ShapeDtypeStruct((3, dh, fh), BF),
        ],
        scratch_shapes=[pltpu.VMEM((2, total, dh), BF)],
        compiler_params=pltpu.CompilerParams(vmem_limit_bytes=LIMIT),
        cost_estimate=pl.CostEstimate(
            flops=2 * total * width * 3 * dh, bytes_accessed=2 * width * 3 * dh, transcendentals=0
        ),
        name="project",
    )(flat, w_qkv, w_rate, f1, f3, f2)


def cross_bits(n, sub):
    bits = [1 << i for i in range(1, n.bit_length() - 1)]
    return bits if sub == 0 else bits[::-1]


def remote(src, dst, send, recv, axis, peer):
    return pltpu.make_async_remote_copy(
        src_ref=src,
        dst_ref=dst,
        send_sem=send,
        recv_sem=recv,
        device_id={axis: peer},
        device_id_type=pl.DeviceIdType.MESH,
    )


def mix_kernel(
    n, nh, blocks, q_ref, kv_ref, g_ref, f1, f3, f2, gain, wo,
    mixed, o1, o3, o2,
    every, half_in, sums, sum_in, total, m_s, l_s, acc, t_buf, t_in,
    h_send, h_recv, d_send, d_recv, a_send, a_recv, k_send, k_recv, r_send, r_recv,
):
    me = lax.axis_index("ctx")
    hme = lax.axis_index("head")
    rows = q_ref.shape[0] // blocks
    dh = q_ref.shape[1]
    reach = WINDOW // rows
    scale = dh ** (-0.5)
    cols = wo.shape[1] // nh
    half = g_ref.shape[1] // 2
    quarter = half // 2
    piece_rows = rows // 2
    core = lax.rem(me, 2)
    mine = pl.multiple_of(core * half, half)
    theirs = pl.multiple_of((1 - core) * half, half)
    levels = n.bit_length() - 2

    barrier = pltpu.get_barrier_semaphore()
    ctx_bits = [1 << i for i in range(n.bit_length() - 1)]
    for bit in ctx_bits:
        pl.semaphore_signal(
            barrier, inc=1, device_id={"ctx": me ^ bit}, device_id_type=pl.DeviceIdType.MESH
        )
    for r in range(1, nh):
        pl.semaphore_signal(
            barrier,
            inc=1,
            device_id={"head": lax.rem(hme + r, nh)},
            device_id_type=pl.DeviceIdType.MESH,
        )
    pl.semaphore_wait(barrier, len(ctx_bits) + nh - 1)

    started = []

    def go(copy):
        copy.start()
        started.append(copy)

    def place(p):
        return pl.ds((p // 2) * rows + (p % 2) * piece_rows, piece_rows)

    def kv_copy(p, c, bit):
        dst = every.at[me ^ c, place(p)]
        src = kv_ref.at[place(p)] if c == 0 else dst
        return remote(
            src, dst, k_send.at[p, c | bit], k_recv.at[p, c | bit], "ctx", me ^ bit
        )

    def kv_wait(p, c):
        dst = every.at[me ^ c, place(p)]
        bit = c & -c
        remote(dst, dst, k_send.at[p, c], k_recv.at[p, c], "ctx", me ^ bit).wait_recv()

    def later(p, c):
        order = cross_bits(n, p % 2)
        last = max([i for i, bit in enumerate(order) if c & bit], default=-1)
        return order[last + 1 :]

    def pass_on(p, c):
        for bit in later(p, c):
            go(kv_copy(p, c, bit))
        go(kv_copy(p, c, 1))

    def first_hop(p):
        return cross_bits(n, p % 2)[0]

    def part(u):
        return pl.ds(u * quarter, quarter)

    def sum_copy(t, u):
        return remote(
            sums.at[t, :, part(u)],
            sum_in.at[t, :, part(u)],
            a_send.at[t, u],
            a_recv.at[t, u],
            "ctx",
            me ^ cross_bits(n, u)[t],
        )

    first = remote(g_ref.at[:, pl.ds(theirs, half)], half_in, h_send, h_recv, "ctx", me ^ 1)
    go(first)
    every[me] = kv_ref[...]
    first.wait_recv()
    sums[0] = (g_ref[:, pl.ds(mine, half)].astype(F32) + half_in[...].astype(F32)).astype(BF)
    for t in range(levels):
        step = [sum_copy(t, u) for u in range(2)]
        for copy in step:
            go(copy)
        if t == levels - 1:
            for p in range(2):
                for bit in cross_bits(n, p):
                    go(kv_copy(p, 0, bit))
            for p in range(2 * blocks):
                go(kv_copy(p, 0, 1))
        for copy in step:
            copy.wait_recv()
        added = (sums[t].astype(F32) + sum_in[t].astype(F32)).astype(BF)
        if t < levels - 1:
            sums[t + 1] = added
        else:
            total[:, pl.ds(mine, half)] = added
    done = total.at[:, pl.ds(mine, half)]
    give = remote(done, done, d_send, d_recv, "ctx", me ^ 1)
    go(give)
    other = total.at[:, pl.ds(theirs, half)]
    remote(other, other, d_send, d_recv, "ctx", me ^ 1).wait_recv()

    for i, x_ref in enumerate((o1, o3, o2)):
        g = total[i].astype(F32)
        x_ref[...] = g * lax.rsqrt(jnp.sum(g * g) + norm_eps)

    def ns_step(_, carry):
        for x_ref in (o1, o3, o2):
            x = x_ref[...]
            xb = x.astype(BF)
            gram = nt(xb, xb)
            gb = gram.astype(BF)
            poly = coeff_b * gram + coeff_c * nn(gb, gb)
            x_ref[...] = coeff_a * x + nn(poly.astype(BF), xb)
        return carry

    early = 3
    lax.fori_loop(0, early, ns_step, 0)
    for p in range(2):
        kv_wait(p, first_hop(p))
        pass_on(p, first_hop(p))
    for p in range(2, 2 * blocks):
        for bit in cross_bits(n, p % 2):
            go(kv_copy(p, 0, bit))
    lax.fori_loop(early, NS_STEPS, ns_step, 0)
    for f, o in ((f1, o1), (f3, o3), (f2, o2)):
        o[...] = f[...] - fast_step * o[...]

    def gather_rest(b):
        pieces = (2 * b, 2 * b + 1)
        evens = sorted(range(2, n, 2), key=lambda c: (bin(c).count("1"), c))
        for c in evens:
            for p in pieces:
                if c != first_hop(p):
                    kv_wait(p, c)
                    pass_on(p, c)
        for c in range(1, n, 2):
            for p in pieces:
                kv_wait(p, c)

    def clear():
        m_s[...] = jnp.full_like(m_s, -1e30)
        l_s[...] = jnp.zeros_like(l_s)
        acc[...] = jnp.zeros_like(acc)

    def attend(b, side):
        here = b * n + me
        q = q_ref[b * rows : (b + 1) * rows]

        def piece(g, carry):
            dev = g - side * n
            k = every[dev, side * rows : (side + 1) * rows, :dh]
            v = every[dev, side * rows : (side + 1) * rows, dh:]
            sc = nt(q, k) * scale
            diff = lax.broadcasted_iota(jnp.int32, (rows, rows), 0) - lax.broadcasted_iota(
                jnp.int32, (rows, rows), 1
            )
            off = diff + (here - g) * rows
            sc = jnp.where((off >= 0) & (off < WINDOW), sc, -1e30)
            old = m_s[...]
            new = jnp.maximum(old, jnp.max(sc, axis=1, keepdims=True))
            p = jnp.where(sc > -1e29, jnp.exp(sc - new), 0.0)
            fade = jnp.exp(old - new)
            l_s[...] = l_s[...] * fade + jnp.sum(p, axis=1, keepdims=True)
            acc[...] = acc[...] * fade + nn(p.astype(BF), v)
            m_s[...] = new
            return carry

        low = jnp.maximum(here - reach, side * n)
        high = jnp.minimum(here, side * n + n - 1)
        lax.fori_loop(low, high + 1, piece, 0)

    def head_copy(b, r):
        peer = lax.rem(hme + r, nh)
        return remote(
            t_buf.at[b, peer],
            t_in.at[b, r - 1],
            r_send.at[b, r - 1],
            r_recv.at[b, r - 1],
            "head",
            peer,
        )

    def finish(b, w1, w3, w2):
        q = q_ref[b * rows : (b + 1) * rows]
        h1 = nn(q, w1[...].astype(BF))
        h3 = nn(q, w3[...].astype(BF))
        act = (jax.nn.silu(h1) * h3).astype(BF)
        out = nn(act, w2[...].astype(BF))
        inv = lax.rsqrt(jnp.mean(out * out, axis=1, keepdims=True) + norm_eps)
        both = (acc[...] / l_s[...] + out * inv * gain[...]).astype(BF)
        for h in range(nh):
            t_buf[b, h] = nn(both, wo[:, h * cols : (h + 1) * cols]).astype(BF)
        copies = [head_copy(b, r) for r in range(1, nh)]
        for copy in copies:
            go(copy)
        return copies

    head_copies = []
    for b in range(blocks):
        clear()
        if b > 0:
            for p in (2 * b, 2 * b + 1):
                kv_wait(p, first_hop(p))
                pass_on(p, first_hop(p))
            attend(b, b - 1)
        gather_rest(b)
        attend(b, b)
        head_copies.append(finish(b, *((f1, f3, f2) if b == 0 else (o1, o3, o2))))
    for b in range(blocks):
        for copy in head_copies[b]:
            copy.wait_recv()
        result = t_buf[b, hme].astype(F32)
        for r in range(nh - 1):
            result = result + t_in[b, r].astype(F32)
        mixed[b] = result.astype(BF)
    for copy in started:
        copy.wait_send()


def mix(n, nh, blocks, q, kv, grads, f1, f3, f2, gain, wo):
    rows = q.shape[0] // blocks
    dh, fh = f1.shape
    cols = wo.shape[1] // nh
    levels = n.bit_length() - 2
    dma = pltpu.SemaphoreType.DMA
    return pl.pallas_call(
        functools.partial(mix_kernel, n, nh, blocks),
        in_specs=[VMEM] * 8,
        out_specs=[VMEM] * 4,
        out_shape=[jax.ShapeDtypeStruct((blocks, rows, cols), BF)]
        + [jax.ShapeDtypeStruct(f.shape, F32) for f in (f1, f3, f2)],
        scratch_shapes=[
            pltpu.VMEM((n,) + kv.shape, BF),
            pltpu.VMEM((3, dh // 2, fh), BF),
            pltpu.VMEM((levels, 3, dh // 2, fh), BF),
            pltpu.VMEM((levels, 3, dh // 2, fh), BF),
            pltpu.VMEM((3, dh, fh), BF),
            pltpu.VMEM((rows, 1), F32),
            pltpu.VMEM((rows, 1), F32),
            pltpu.VMEM((rows, dh), F32),
            pltpu.VMEM((blocks, nh, rows, cols), BF),
            pltpu.VMEM((blocks, nh - 1, rows, cols), BF),
            dma,
            dma,
            dma,
            dma,
            dma((levels, 2)),
            dma((levels, 2)),
            dma((2 * blocks, n)),
            dma((2 * blocks, n)),
            dma((blocks, nh - 1)),
            dma((blocks, nh - 1)),
        ],
        compiler_params=pltpu.CompilerParams(
            vmem_limit_bytes=63 * 1024 * 1024, collective_id=0, has_side_effects=True
        ),
        name="mix",
    )(q, kv, grads, f1, f3, f2, gain, wo)


def shards(tokens, w_qkv, w_rate, w_out, fw_gain, fast_first, fast_third, fast_second):
    blocks, rows, width = tokens.shape
    dh = w_out.shape[1]
    n_ctx = lax.axis_size("ctx")
    flat = tokens.reshape(blocks * rows, width)
    fast = (fast_first[0], fast_third[0], fast_second[0])
    q, kv, grads = project(
        flat, rows, w_qkv.reshape(width, 3 * dh), w_rate.reshape(1, width), *fast
    )
    mixed, *current = mix(
        n_ctx, lax.axis_size("head"), blocks, q, kv, grads, *fast, fw_gain, w_out[0]
    )
    return (mixed,) + tuple(f[None] for f in current)


def solution(mesh):
    placed = (
        P(None, "ctx", None),
        P(None, "head", None),
        P(None, "head"),
        P("head", None, None),
        P("head", None),
        P("head", None, None),
        P("head", None, None),
        P("head", None, None),
    )
    return jax.shard_map(
        shards,
        mesh=mesh,
        in_specs=placed,
        out_specs=(
            P(None, "ctx", "head"),
            P("head", None, None),
            P("head", None, None),
            P("head", None, None),
        ),
        check_vma=False,
    )
```

profile of v0, /device:TPU:10, one launch (start us, length us, event | category | flops | bytes accessed | tf_op | source)
XLA Modules:
  0.0 120.9 jit_solution(933908815258900187)
XLA Ops:
  0.6 10.5 %project.1 = (bf16[512,512]{1,0:T(8,128)(2,1)}, bf16[512,1024]{1,0:T(8,128)(2,1)}, bf16[3,512,512]{2,1,0:T(8,128)(2,1)}) custom-call(bf16[512,2048]{1,0:T(8,128)(2,1)} %bitcast.21, bf16[2048,1536]{1,0:T(8,128)(2,1)} %bitcast.20, bf16[1,2048]{1,0:T(2,128)(2,1)} %bitcast.22, f32[512,512]{1,0:T(8,128)} %bitcast.11, f32[512,512]{1,0:T(8,128)} %bitcast.13, ...), custom_call_target="tpu_custom_call" | custom-call | flops 3221225472 | bytes 6291456 | tf_op jit(solution)/shard_map/project/pallas_call | solution.py:77
  11.1 103.5 %mix.1 = (bf16[2,256,512]{2,1,0:T(8,128)(2,1)}, f32[512,512]{1,0:T(8,128)}, f32[512,512]{1,0:T(8,128)}, f32[512,512]{1,0:T(8,128)}) custom-call(bf16[512,512]{1,0:T(8,128)(2,1)} %get-tuple-element.11.q_ref, bf16[512,1024]{1,0:T(8,128)(2,1)} %get-tuple-element.12.kv_ref, bf16[3,512,512]{2,1,0:T(8,128)(2,1)} %get-tuple-element.13.g_ref, f32[512,512]{1,0:T(8,128)} %bitcast.12, ...), custom_call_target="tpu_custom_call" | custom-call | tf_op jit(solution)/shard_map/mix/pallas_call | solution.py:358
  114.7 0.0 copy-start.1
  114.7 2.0 %copy.16 = bf16[2,256,512]{2,1,0:T(8,128)(2,1)} copy(bf16[2,256,512]{2,1,0:T(8,128)(2,1)} %get-tuple-element.22) | data formatting | bytes 1048576
  116.6 0.0 copy-start
  116.6 2.4 %copy.17 = f32[1,512,512]{2,1,0:T(8,128)} copy(f32[1,512,512]{2,1,0:T(8,128)} %bitcast.19) | data formatting | bytes 2097152
  119.0 0.0 copy-done.1
  119.0 1.0 copy.18
  120.0 0.0 copy-done
  120.0 1.0 copy.19
Async XLA Ops:
  114.7 4.3 %copy-start.1 = (f32[512,512]{1,0:T(8,128)S(1)}, f32[512,512]{1,0:T(8,128)}, u32[]{:S(2)}) copy-start(f32[512,512]{1,0:T(8,128)} %get-tuple-element.16) | copy-start | bytes 3145732
  116.6 3.3 %copy-start = (f32[512,512]{1,0:T(8,128)S(1)}, f32[512,512]{1,0:T(8,128)}, u32[]{:S(2)}) copy-start(f32[512,512]{1,0:T(8,128)} %get-tuple-element.17) | copy-start | bytes 3145732
where the time goes:
time: 123 us; the launch traced here: 121 us
  Pallas kernels  114 us (93%)
  local copies, waits for them, and re-layouts  6.25 us (5%)
    pallas_call x1, Pallas kernels, mix(): pl.pallas_call(functools.partial(mix_kernel, n, nh, blocks), in_specs=[VM...  104 us
    pallas_call x1, Pallas kernels, project(): pl.pallas_call(functools.partial(project_kernel, rows), grid=(3,), in_spe...  10.5 us
    unnamed x8, local copies, waits for them, and re-layouts  6.25 us

commit v1 on v0

v1 whole, which is shorter than its diff:
```python
import functools

import jax
import jax.numpy as jnp
from jax import lax
from jax.experimental import pallas as pl
from jax.experimental.pallas import tpu as pltpu
from jax.sharding import PartitionSpec as P

WINDOW = 2048
NS_STEPS = 5

coeff_a = 3.4445
coeff_b = -4.775
coeff_c = 2.0315
fast_step = 0.5
norm_eps = 1e-06
LOG2E = 1.4426950408889634
NEG = -1e30
BF = jnp.bfloat16
F32 = jnp.float32
VMEM = pl.BlockSpec(memory_space=pltpu.VMEM)
ANY = pl.BlockSpec(memory_space=pl.ANY)
LANES = 128


def mm(left, right, dims):
    return lax.dot_general(left, right, (dims, ((), ())), preferred_element_type=F32)


def nn(left, right):
    return mm(left, right, ((1,), (0,)))


def nt(left, right):
    return mm(left, right, ((1,), (1,)))


def tn(left, right):
    return mm(left, right, ((0,), (0,)))


def cross_bits(n, sub):
    bits = [1 << i for i in range(1, n.bit_length() - 1)]
    return bits if sub == 0 else bits[::-1]


def remote(src, dst, send, recv, axis, peer):
    return pltpu.make_async_remote_copy(
        src_ref=src,
        dst_ref=dst,
        send_sem=send,
        recv_sem=recv,
        device_id={axis: peer},
        device_id_type=pl.DeviceIdType.MESH,
    )


def layer_kernel(
    n, nh, rows,
    tok_h, w_h, wr, f1_h, f3_h, f2_h, gain, wo_h,
    mixed_h, o1_h, o3_h, o2_h,
    tok, w, f_v, fb, wo, wp, q_v, every, rates,
    grad, g_out, g_in,
    m_s, l_s, acc, normed, comb, part_in, res,
    load, k_send, k_recv, s_send, s_recv, g_send, g_recv, x_send, x_recv,
    w_send, w_recv, c_send, c_recv, p_send, p_recv, out_sem,
):
    me = lax.axis_index("ctx")
    hme = lax.axis_index("head")
    dh = q_v.shape[1]
    cols = wo.shape[2]
    reach = WINDOW // rows
    scale = dh ** (-0.5) * LOG2E
    half = rows // 2
    core = lax.rem(me, 2)
    fine = n <= 8
    evens = sorted(range(2, n, 2), key=lambda c: (bin(c).count("1"), c))
    hpair = hme // 2
    hodd = lax.rem(hme, 2)
    mate = hme + 1 - 2 * hodd

    def fetch(i, src, dst):
        copy = pltpu.make_async_copy(src, dst, load.at[i])
        copy.start()
        return copy

    first, second = pl.ds(0, rows), pl.ds(rows, rows)
    in_tok0 = fetch(0, tok_h.at[first], tok.at[first])
    in_k = fetch(1, w_h.at[:, pl.ds(dh, dh)], w.at[1])
    in_v = fetch(2, w_h.at[:, pl.ds(2 * dh, dh)], w.at[2])
    in_tok1 = fetch(3, tok_h.at[second], tok.at[second])
    in_q = fetch(4, w_h.at[:, pl.ds(0, dh)], w.at[0])
    in_f = [fetch(5 + i, f, f_v.at[i]) for i, f in enumerate((f1_h, f3_h, f2_h))]
    in_wo = [
        fetch(8 + t, wo_h.at[:, pl.ds(t * cols, cols)], wo.at[t]) for t in range(nh)
    ]

    barrier = pltpu.get_barrier_semaphore()
    peers = [1] + evens
    for c in peers:
        pl.semaphore_signal(
            barrier, inc=1, device_id={"ctx": me ^ c}, device_id_type=pl.DeviceIdType.MESH
        )
    for r in range(1, nh):
        pl.semaphore_signal(
            barrier,
            inc=1,
            device_id={"head": lax.rem(hme + r, nh)},
            device_id_type=pl.DeviceIdType.MESH,
        )

    started = []

    def go(copy):
        copy.start()
        started.append(copy)

    def place(p):
        return pl.ds((p // 2) * rows + (p % 2) * half, half)

    def kv_copy(p, c, bit):
        ref = every.at[me ^ c, place(p)]
        return remote(ref, ref, k_send.at[p, c | bit], k_recv.at[p, c | bit], "ctx", me ^ bit)

    def kv_wait(p, c):
        ref = every.at[me ^ c, place(p)]
        remote(ref, ref, k_send.at[p, c], k_recv.at[p, c], "ctx", me ^ (c & -c)).wait_recv()

    def pass_on(p, c):
        order = cross_bits(n, p % 2)
        last = max(i for i, bit in enumerate(order) if c & bit)
        for bit in order[last + 1 :]:
            go(kv_copy(p, c, bit))
        go(kv_copy(p, c, 1))

    def send_own(b):
        lists = [cross_bits(n, sub) for sub in range(2)]
        for pair in zip(*lists):
            for sub in range(2):
                go(kv_copy(2 * b + sub, 0, pair[sub]))
        for sub in range(2):
            go(kv_copy(2 * b + sub, 0, 1))

    def first_hops(b):
        for sub in range(2):
            c = cross_bits(n, sub)[0]
            kv_wait(2 * b + sub, c)
            pass_on(2 * b + sub, c)

    def near_hops(b):
        for sub in range(2):
            for c in evens:
                if c & (c - 1) == 0 and c != cross_bits(n, sub)[0]:
                    kv_wait(2 * b + sub, c)
                    pass_on(2 * b + sub, c)

    def far_hops(b):
        for c in evens:
            if c & (c - 1):
                for sub in range(2):
                    kv_wait(2 * b + sub, c)
                    pass_on(2 * b + sub, c)

    def from_mate(b, c):
        for sub in range(2):
            kv_wait(2 * b + sub, c)

    in_tok0.wait()
    in_k.wait()
    every[me, :rows, :dh] = nn(tok[:rows], w[1]).astype(BF)
    in_v.wait()
    every[me, :rows, dh:] = nn(tok[:rows], w[2]).astype(BF)
    pl.semaphore_wait(barrier, len(peers) + nh - 1)
    send_own(0)

    logit = nt(jnp.broadcast_to(wr[...], (8, wr.shape[1])), tok[:rows])
    rates[0] = jnp.maximum(logit, 0.0) + jnp.log1p(jnp.exp(-jnp.abs(logit)))
    for c in evens:
        go(
            remote(
                rates.at[0], rates.at[c // 2], s_send.at[c // 2], s_recv.at[c // 2], "ctx", me ^ c
            )
        )

    def rate_wait(c):
        ref = rates.at[c // 2]
        remote(ref, ref, s_send.at[c // 2], s_recv.at[c // 2], "ctx", me ^ c).wait_recv()

    def crosses(h, t):
        odd = lax.rem(h, 2)
        up = (odd == 1) & (t // 2 > h // 2)
        down = (odd == 0) & (t // 2 < h // 2)
        return up | down

    def wo_copy(t):
        return remote(
            wo_h.at[:, pl.ds(t * cols, cols)], wp.at[t], w_send.at[t], w_recv.at[t], "head", mate
        )

    for t in range(nh):

        @pl.when((mate == t) | crosses(mate, t))
        def _():
            wo_copy(t).start()

    in_tok1.wait()
    every[me, rows:, :dh] = nn(tok[rows:], w[1]).astype(BF)
    every[me, rows:, dh:] = nn(tok[rows:], w[2]).astype(BF)
    in_q.wait()
    q_v[...] = nn(tok[...], w[0]).astype(BF)
    for i in range(3):
        in_f[i].wait()
        fb[i] = f_v[i].astype(BF)

    def gradients(s, at, slot, add):
        keys = every[s, :rows, :dh]
        vals = every[s, :rows, dh:]
        rate = jnp.transpose(rates[at])[:, :1]
        target = (-rate * vals.astype(F32)).astype(BF)
        h1 = nn(keys, fb[0])
        h3 = nn(keys, fb[1])
        sig = jax.nn.sigmoid(h1)
        silu = h1 * sig
        act = (silu * h3).astype(BF)
        dact = nt(target, fb[2])
        d1 = (dact * h3 * (sig * (1.0 + h1 * (1.0 - sig)))).astype(BF)
        d3 = (dact * silu).astype(BF)
        new = (tn(keys, d1), tn(keys, d3), tn(act, target))
        for i in range(3):
            grad[slot, i] = grad[slot, i] + new[i] if add else new[i]

    def attend(b, s, side, gap, begin=False):
        q = q_v[pl.ds(pl.multiple_of(b * rows, rows), rows)]
        k = every[s, side * rows : (side + 1) * rows, :dh]
        v = every[s, side * rows : (side + 1) * rows, dh:]
        diff = lax.broadcasted_iota(jnp.int32, (rows, rows), 0) - lax.broadcasted_iota(
            jnp.int32, (rows, rows), 1
        )
        off = diff + gap * rows
        sc = jnp.where((off >= 0) & (off < WINDOW), nt(q, k), NEG)
        top = jnp.max(sc, axis=1, keepdims=True)
        new = top if begin else jnp.maximum(m_s[b], top)
        p = jnp.exp2((sc - new) * scale)
        lane = sum(p[:, i : i + LANES] for i in range(0, rows, LANES))
        pv = nn(p.astype(BF), v)
        if begin:
            l_s[b] = lane
            acc[b] = pv
        else:
            fade = jnp.exp2((m_s[b] - new) * scale)
            l_s[b] = l_s[b] * fade + lane
            acc[b] = acc[b] * fade + pv
        m_s[b] = new

    def visit(side, s):
        gap = me - s
        if side == 0:
            b = jnp.where(gap >= 0, 0, 1)
            gap = gap + b * n

            @pl.when(gap <= reach)
            def _():
                attend(b, s, 0, gap)
        else:

            @pl.when((gap >= 0) & (gap <= reach))
            def _():
                attend(1, s, 1, gap)

    def visit_all(side):
        def one(s, carry):
            @pl.when(s != me)
            def _():
                visit(side, s)

            return carry

        lax.fori_loop(0, n, one, 0)

    if fine:
        gradients(me, 0, 0, False)
    first_hops(0)
    send_own(1)
    attend(0, me, 0, 0, True)
    attend(1, me, 1, 0, True)

    if n <= reach:
        attend(1, me, 0, n)

    from_mate(0, 1)
    if fine:
        visit(0, me ^ 1)
    near_hops(0)
    for c in evens:
        rate_wait(c)
    if fine:
        for c in evens:
            if c & (c - 1) == 0:
                gradients(me ^ c, c // 2, c // 4, c < 4)
        for c in evens:
            if c & (c - 1) == 0:
                visit(0, me ^ c)
    far_hops(0)
    if fine:
        for c in evens:
            if c & (c - 1):
                gradients(me ^ c, c // 2, 1, True)
        slots = 2 if n > 4 else 1
    else:
        grad[0] = jnp.zeros_like(grad[0])

        def summed(j, carry):
            gradients(2 * j + core, (me // 2) ^ j, 0, True)
            return carry

        lax.fori_loop(0, n // 2, summed, 0)
        slots = 1

    def total(i):
        return grad[0, i] + grad[1, i] if slots == 2 else grad[0, i]

    def g_copy(i):
        return remote(g_out.at[i], g_in.at[i], g_send.at[i], g_recv.at[i], "ctx", me ^ 1)

    def x_copy(i):
        return remote(g_out.at[i], g_in.at[i], x_send.at[i], x_recv.at[i], "ctx", me ^ 1)

    owned = ((0, 1), (2,))

    for own in range(2):

        @pl.when(core == own)
        def _():
            for i in owned[1 - own]:
                g_out[i] = total(i).astype(BF)
                g_copy(i).start()

    def fast_out(b, weights):
        q = q_v[b * rows : (b + 1) * rows]
        h1 = nn(q, weights[0])
        h3 = nn(q, weights[1])
        act = (jax.nn.silu(h1) * h3).astype(BF)
        out = nn(act, weights[2])
        inv = lax.rsqrt(jnp.mean(out * out, axis=1, keepdims=True) + norm_eps)
        normed[...] = out * inv * gain[...]

    chunks = comb.shape[2]
    step = rows // chunks

    def c_copy(b, u):
        return remote(
            comb.at[b, 0, u], comb.at[b, 1, u], c_send.at[b, u], c_recv.at[b, u], "head", mate
        )

    def spot(b, u):
        return pl.ds(b * rows + u * step, step)

    def p_copy(b, u, t):
        return remote(
            tok.at[spot(b, u), pl.ds(t * cols, cols)],
            part_in.at[b, hpair, u],
            p_send.at[b, u, t],
            p_recv.at[b, u, hpair],
            "head",
            t,
        )

    def combine(b):
        both = acc[b] / jnp.sum(l_s[b], axis=1, keepdims=True) + normed[...]
        for u in range(chunks):
            comb[b, 0, u] = both[u * step : (u + 1) * step].astype(BF)
            go(c_copy(b, u))

    def cross(b):
        for u in range(chunks):
            c_copy(b, u).wait_recv()
            for t in range(nh):

                @pl.when(crosses(hme, t))
                def _():
                    tok[spot(b, u), t * cols : (t + 1) * cols] = (
                        nn(comb[b, 0, u], wo[t]) + nn(comb[b, 1, u], wp[t])
                    ).astype(BF)
                    p_copy(b, u, t).start()

        for u in range(chunks):
            res[b, u * step : (u + 1) * step] = nn(comb[b, 0, u], wo[hme]) + nn(
                comb[b, 1, u], wp[hme]
            )

    def close(b):
        for u in range(chunks):
            for pair in range(nh // 2):

                @pl.when(hpair != pair)
                def _():
                    ref = part_in.at[b, pair, u]
                    remote(
                        ref, ref, p_send.at[b, u, 0], p_recv.at[b, u, pair], "head", mate
                    ).wait_recv()
                    here = slice(u * step, (u + 1) * step)
                    res[b, here] = res[b, here] + part_in[b, pair, u].astype(F32)

        q_v[b * rows : (b + 1) * rows] = res[b].astype(BF)
        copy = pltpu.make_async_copy(
            q_v.at[pl.ds(b * rows, rows)], mixed_h.at[b], out_sem.at[3 + b]
        )
        copy.start()
        return copy

    if fine:
        for c in evens:
            if c & (c - 1) == 0:
                from_mate(0, c + 1)
                visit(0, me ^ (c + 1))
        for c in evens:
            if c & (c - 1):
                visit(0, me ^ c)
                from_mate(0, c + 1)
                visit(0, me ^ (c + 1))
    else:
        for c in evens:
            from_mate(0, c + 1)
        visit_all(0)
    fast_out(0, fb)
    for copy in in_wo:
        copy.wait()
    combine(0)

    def ns_steps(mats, count):
        def one(_, carry):
            for i in mats:
                x = grad[0, i]
                xb = x.astype(BF)
                gram = nt(xb, xb)
                gb = gram.astype(BF)
                poly = coeff_b * gram + coeff_c * nn(gb, gb)
                grad[0, i] = coeff_a * x + nn(poly.astype(BF), xb)
            return carry

        lax.fori_loop(0, count, one, 0)

    for own in range(2):

        @pl.when(core == own)
        def _():
            for i in owned[own]:
                g_copy(i).wait_recv()
                g = total(i) + g_in[i].astype(F32)
                grad[0, i] = g * lax.rsqrt(jnp.sum(g * g) + norm_eps)
            ns_steps(owned[own], 1)

    first_hops(1)
    for own in range(2):

        @pl.when(core == own)
        def _():
            ns_steps(owned[own], NS_STEPS - 1)
            for i in owned[own]:
                g_out[i] = grad[0, i].astype(BF)
                x_copy(i).start()

    near_hops(1)
    for t in range(nh):

        @pl.when((hme == t) | crosses(hme, t))
        def _():
            wo_copy(t).wait_recv()

    cross(0)
    from_mate(1, 1)
    if fine:
        visit(1, me ^ 1)
        for c in evens:
            if c & (c - 1) == 0:
                visit(1, me ^ c)
                from_mate(1, c + 1)
                visit(1, me ^ (c + 1))

    outs = (o1_h, o3_h, o2_h)
    for own in range(2):

        @pl.when(core == own)
        def _():
            for i in owned[1 - own]:
                x_copy(i).wait_recv()
                new = f_v[i] - fast_step * g_in[i].astype(F32)
                f_v[i] = new
                fb[i] = new.astype(BF)
            for i in owned[own]:
                new = f_v[i] - fast_step * g_out[i].astype(F32)
                f_v[i] = new
                fb[i] = new.astype(BF)

    writes = [pltpu.make_async_copy(f_v.at[i], outs[i], out_sem.at[i]) for i in range(3)]
    for copy in writes:
        copy.start()
    fast_out(1, fb)
    far_hops(1)
    if fine:
        for c in evens:
            if c & (c - 1):
                visit(1, me ^ c)
                from_mate(1, c + 1)
                visit(1, me ^ (c + 1))
    else:
        for c in evens:
            from_mate(1, c + 1)
        visit_all(1)
    combine(1)
    writes.append(close(0))
    cross(1)
    writes.append(close(1))
    for copy in writes:
        copy.wait()
    for copy in started:
        copy.wait_send()
    for own in range(2):

        @pl.when(core == own)
        def _():
            for i in owned[1 - own]:
                g_copy(i).wait_send()
            for i in owned[own]:
                x_copy(i).wait_send()

    for t in range(nh):

        @pl.when((mate == t) | crosses(mate, t))
        def _():
            wo_copy(t).wait_send()

        @pl.when(crosses(hme, t))
        def _():
            for b in range(2):
                for u in range(chunks):
                    p_copy(b, u, t).wait_send()


def layer(n, nh, rows, flat, w_qkv, w_rate, f1, f3, f2, gain, wo):
    total, width = flat.shape
    blocks = total // rows
    dh, fh = f1.shape
    cols = wo.shape[1] // nh
    chunks = 2
    step = rows // chunks
    dma = pltpu.SemaphoreType.DMA
    return pl.pallas_call(
        functools.partial(layer_kernel, n, nh, rows),
        in_specs=[ANY, ANY, VMEM, ANY, ANY, ANY, VMEM, ANY],
        out_specs=[ANY] * 4,
        out_shape=[jax.ShapeDtypeStruct((blocks, rows, cols), BF)]
        + [jax.ShapeDtypeStruct(f.shape, F32) for f in (f1, f3, f2)],
        scratch_shapes=[
            pltpu.VMEM((total, width), BF),
            pltpu.VMEM((3, width, dh), BF),
            pltpu.VMEM((3, dh, fh), F32),
            pltpu.VMEM((3, dh, fh), BF),
            pltpu.VMEM((nh, dh, cols), BF),
            pltpu.VMEM((nh, dh, cols), BF),
            pltpu.VMEM((total, dh), BF),
            pltpu.VMEM((n, total, 2 * dh), BF),
            pltpu.VMEM((n // 2, 8, rows), F32),
            pltpu.VMEM((2 if n <= 8 else 1, 3, dh, fh), F32),
            pltpu.VMEM((3, dh, fh), BF),
            pltpu.VMEM((3, dh, fh), BF),
            pltpu.VMEM((blocks, rows, 1), F32),
            pltpu.VMEM((blocks, rows, LANES), F32),
            pltpu.VMEM((blocks, rows, dh), F32),
            pltpu.VMEM((rows, dh), F32),
            pltpu.VMEM((blocks, 2, chunks, step, dh), BF),
            pltpu.VMEM((blocks, nh // 2, chunks, step, cols), BF),
            pltpu.VMEM((blocks, rows, cols), F32),
            dma((8 + nh,)),
            dma((2 * blocks, n)),
            dma((2 * blocks, n)),
            dma((n // 2,)),
            dma((n // 2,)),
            dma((3,)),
            dma((3,)),
            dma((3,)),
            dma((3,)),
            dma((nh,)),
            dma((nh,)),
            dma((blocks, chunks)),
            dma((blocks, chunks)),
            dma((blocks, chunks, nh)),
            dma((blocks, chunks, nh // 2)),
            dma((3 + blocks,)),
        ],
        compiler_params=pltpu.CompilerParams(
            vmem_limit_bytes=67_000_000, collective_id=0, has_side_effects=True
        ),
        name="layer",
    )(flat, w_qkv, w_rate, f1, f3, f2, gain, wo)


def shards(tokens, w_qkv, w_rate, w_out, fw_gain, fast_first, fast_third, fast_second):
    blocks, rows, width = tokens.shape
    dh = w_out.shape[1]
    mixed, *current = layer(
        lax.axis_size("ctx"),
        lax.axis_size("head"),
        rows,
        tokens.reshape(blocks * rows, width),
        w_qkv.reshape(width, 3 * dh),
        w_rate.reshape(1, width),
        fast_first[0],
        fast_third[0],
        fast_second[0],
        fw_gain,
        w_out[0],
    )
    return (mixed,) + tuple(f[None] for f in current)


def solution(mesh):
    placed = (
        P(None, "ctx", None),
        P(None, "head", None),
        P(None, "head"),
        P("head", None, None),
        P("head", None),
        P("head", None, None),
        P("head", None, None),
        P("head", None, None),
    )
    return jax.shard_map(
        shards,
        mesh=mesh,
        in_specs=placed,
        out_specs=(
            P(None, "ctx", "head"),
            P("head", None, None),
            P("head", None, None),
            P("head", None, None),
        ),
        check_vma=False,
    )
```

time: 123 us -> 78.6 us (0.64)
  Pallas kernels: 114 us -> 70.4 us
    pallas_call x2 -> x1, Pallas kernels: 114 us -> 70.4 us  [layer(): pl.pallas_call(functools.partial(layer_kernel, n, nh, rows), in_specs=[AN...]
where the time goes in v1:
time: 78.6 us; the launch traced here: 77.3 us
  Pallas kernels  70.4 us (90%)
  local copies, waits for them, and re-layouts  6.25 us (8%)
    pallas_call x1, Pallas kernels, layer(): pl.pallas_call(functools.partial(layer_kernel, n, nh, rows), in_specs=[AN...  70.4 us
    unnamed x8, local copies, waits for them, and re-layouts  6.25 us

profile of v1, /device:TPU:10, one launch (start us, length us, event | category | flops | bytes accessed | tf_op | source)
XLA Modules:
  0.0 77.3 jit_solution(13351195257627998116)
XLA Ops:
  0.6 70.4 %layer.1 = (bf16[2,256,512]{2,1,0:T(8,128)(2,1)}, f32[512,512]{1,0:T(8,128)}, f32[512,512]{1,0:T(8,128)}, f32[512,512]{1,0:T(8,128)}) custom-call(bf16[512,2048]{1,0:T(8,128)(2,1)} %bitcast.11, bf16[2048,1536]{1,0:T(8,128)(2,1)} %bitcast.10, bf16[1,2048]{1,0:T(2,128)(2,1)} %bitcast.19, f32[512,512]{1,0:T(8,128)} %bitcast.13, f32[512,512]{1,0:T(8,128)} %bitcast.14, ...), custom_call_target="tpu_custom_call" | custom-call | tf_op jit(solution)/shard_map/layer/pallas_call | solution.py:549
  71.0 0.0 copy-start.1
  71.0 2.0 %copy.16 = bf16[2,256,512]{2,1,0:T(8,128)(2,1)} copy(bf16[2,256,512]{2,1,0:T(8,128)(2,1)} %get-tuple-element.16) | data formatting | bytes 1048576
  73.0 0.0 copy-start
  73.0 2.4 %copy.17 = f32[1,512,512]{2,1,0:T(8,128)} copy(f32[1,512,512]{2,1,0:T(8,128)} %bitcast.18) | data formatting | bytes 2097152
  75.3 0.0 copy-done.1
  75.3 1.0 %copy.18 = f32[1,512,512]{2,1,0:T(8,128)} copy(f32[1,512,512]{2,1,0:T(8,128)S(1)} %bitcast.17) | data formatting | bytes 2097152
  76.3 0.0 copy-done
  76.3 1.0 %copy.19 = f32[1,512,512]{2,1,0:T(8,128)} copy(f32[1,512,512]{2,1,0:T(8,128)S(1)} %bitcast.16) | data formatting | bytes 2097152
Async XLA Ops:
  71.0 4.3 %copy-start.1 = (f32[512,512]{1,0:T(8,128)S(1)}, f32[512,512]{1,0:T(8,128)}, u32[]{:S(2)}) copy-start(f32[512,512]{1,0:T(8,128)} %get-tuple-element.10) | copy-start | bytes 3145732
  73.0 3.3 %copy-start = (f32[512,512]{1,0:T(8,128)S(1)}, f32[512,512]{1,0:T(8,128)}, u32[]{:S(2)}) copy-start(f32[512,512]{1,0:T(8,128)} %get-tuple-element.11) | copy-start | bytes 3145732

commit v2 on v1

v2 whole, which is shorter than its diff:
```python
import functools
import math

import jax
import jax.numpy as jnp
from jax import lax
from jax.experimental import pallas as pl
from jax.experimental.pallas import tpu as pltpu
from jax.sharding import PartitionSpec as P

WINDOW = 2048
NS_STEPS = 5

coeff_a = 3.4445
coeff_b = -4.775
coeff_c = 2.0315
fast_step = 0.5
norm_eps = 1e-06
LOG2E = 1.4426950408889634
NEG = -1e30
BF = jnp.bfloat16
F32 = jnp.float32
VMEM = pl.BlockSpec(memory_space=pltpu.VMEM)
ANY = pl.BlockSpec(memory_space=pl.ANY)
HBM = pl.BlockSpec(memory_space=pltpu.HBM)
LANES = 128


def mm(left, right, dims):
    return lax.dot_general(left, right, (dims, ((), ())), preferred_element_type=F32)


def nn(left, right):
    return mm(left, right, ((1,), (0,)))


def nt(left, right):
    return mm(left, right, ((1,), (1,)))


def tn(left, right):
    return mm(left, right, ((0,), (0,)))


def cross_bits(n, sub):
    bits = [1 << i for i in range(1, n.bit_length() - 1)]
    return bits if sub == 0 else bits[::-1]


def remote(src, dst, send, recv, axis, peer):
    return pltpu.make_async_remote_copy(
        src_ref=src,
        dst_ref=dst,
        send_sem=send,
        recv_sem=recv,
        device_id={axis: peer},
        device_id_type=pl.DeviceIdType.MESH,
    )


def layer_kernel(
    n, nh, rows,
    tok_h, w_h, wr_h, f1_h, f3_h, f2_h, gain_h, wo_h,
    mixed_h, o1_h, o3_h, o2_h,
    tok, w, wr, gain, f_v, fb, wo, wp, q_v, every, rates,
    grad, g_out, g_in,
    m_s, l_s, acc, normed, comb, part_in, res,
    load, k_send, k_recv, s_send, s_recv, g_send, g_recv, x_send, x_recv,
    w_send, w_recv, c_send, c_recv, p_send, p_recv, out_sem,
):
    me = lax.axis_index("ctx")
    hme = lax.axis_index("head")
    dh = q_v.shape[1]
    cols = wo.shape[2]
    reach = WINDOW // rows
    scale = dh ** (-0.5) * LOG2E
    core = lax.rem(me, 2)
    fine = n <= 8
    evens = sorted(range(2, n, 2), key=lambda c: (bin(c).count("1"), c))
    hpair = hme // 2
    hodd = lax.rem(hme, 2)
    mate = hme + 1 - 2 * hodd

    def fetch(i, src, dst):
        copy = pltpu.make_async_copy(src, dst, load.at[i])
        copy.start()
        return copy

    first, second = pl.ds(0, rows), pl.ds(rows, rows)
    in_tok0 = fetch(0, tok_h.at[first], tok.at[first])
    in_k = fetch(1, w_h.at[:, pl.ds(dh, dh)], w.at[1])

    barrier = pltpu.get_barrier_semaphore()
    peers = [1] + evens
    for c in peers:
        pl.semaphore_signal(
            barrier, inc=1, device_id={"ctx": me ^ c}, device_id_type=pl.DeviceIdType.MESH
        )
    for r in range(1, nh):
        pl.semaphore_signal(
            barrier,
            inc=1,
            device_id={"head": lax.rem(hme + r, nh)},
            device_id_type=pl.DeviceIdType.MESH,
        )

    started = []

    def go(make):
        make().start()
        started.append(make)

    half = rows // 2

    def piece(p, c):
        b, kv, sub = p // 4, p // 2 % 2, p % 2
        return every.at[me ^ c, kv, pl.ds(b * rows + sub * half, half)]

    def pieces(b):
        return [(4 * b + 2 * kv + sub, sub) for kv in range(2) for sub in range(2)]

    def kv_copy(p, c, bit):
        ref = piece(p, c)
        return remote(ref, ref, k_send.at[p, c | bit], k_recv.at[p, c | bit], "ctx", me ^ bit)

    def kv_wait(p, c):
        ref = piece(p, c)
        remote(ref, ref, k_send.at[p, c], k_recv.at[p, c], "ctx", me ^ (c & -c)).wait_recv()

    def pass_on(p, c):
        order = cross_bits(n, p % 2)
        last = max(i for i, bit in enumerate(order) if c & bit)
        for bit in order[last + 1 :]:
            go(functools.partial(kv_copy, p, c, bit))
        go(functools.partial(kv_copy, p, c, 1))

    def send_own(b, kv, turns):
        for turn in turns:
            for sub in range(2):
                bits = cross_bits(n, sub)
                go(functools.partial(kv_copy, 4 * b + 2 * kv + sub, 0, bits[turn]))
        if 0 in turns:
            for sub in range(2):
                go(functools.partial(kv_copy, 4 * b + 2 * kv + sub, 0, 1))

    later_turns = range(1, len(cross_bits(n, 0)))

    def hops(b, far, first):
        for c in evens:
            for p, sub in pieces(b):
                if far == (c & (c - 1) != 0) and (far or first == (c == cross_bits(n, sub)[0])):
                    kv_wait(p, c)
                    pass_on(p, c)

    def first_hops(b):
        hops(b, False, True)

    def near_hops(b):
        hops(b, False, False)

    def far_hops(b):
        hops(b, True, False)

    def from_mate(b, c):
        for p, _ in pieces(b):
            kv_wait(p, c)

    in_tok0.wait()
    in_k.wait()
    in_v = fetch(2, w_h.at[:, pl.ds(2 * dh, dh)], w.at[2])
    in_wr = fetch(8 + nh, wr_h, wr)
    in_gain = fetch(9 + nh, gain_h, gain)
    every[me, 0, :rows] = nn(tok[:rows], w[1]).astype(BF)
    pl.semaphore_wait(barrier, len(peers) + nh - 1)
    send_own(0, 0, (0,))
    in_v.wait()
    in_tok1 = fetch(3, tok_h.at[second], tok.at[second])
    in_q = fetch(4, w_h.at[:, pl.ds(0, dh)], w.at[0])
    in_f = [fetch(5 + i, f, f_v.at[i]) for i, f in enumerate((f1_h, f3_h, f2_h))]
    in_wo = [
        fetch(8 + t, wo_h.at[:, pl.ds(t * cols, cols)], wo.at[t]) for t in range(nh)
    ]
    every[me, 1, :rows] = nn(tok[:rows], w[2]).astype(BF)
    send_own(0, 1, (0,))
    for kv in range(2):
        send_own(0, kv, later_turns)

    def rate_copy(c):
        i = c // 2
        return remote(rates.at[0], rates.at[i], s_send.at[i], s_recv.at[i], "ctx", me ^ c)

    in_wr.wait()
    logit = nt(jnp.broadcast_to(wr[...], (8, wr.shape[1])), tok[:rows])
    rates[0] = jnp.maximum(logit, 0.0) + jnp.log1p(jnp.exp(-jnp.abs(logit)))
    for c in evens:
        go(functools.partial(rate_copy, c))

    def crosses(h, t):
        odd = lax.rem(h, 2)
        up = (odd == 1) & (t // 2 > h // 2)
        down = (odd == 0) & (t // 2 < h // 2)
        return up | down

    share = pl.ds(pl.multiple_of(core * (dh // 2), dh // 2), dh // 2)

    def wo_copy(t):
        return remote(
            wo_h.at[share, pl.ds(t * cols, cols)],
            wp.at[t, share],
            w_send.at[0, t],
            w_recv.at[0, t],
            "head",
            mate,
        )

    def wo_pass(t):
        ref = wp.at[t, share]
        return remote(ref, ref, w_send.at[1, t], w_recv.at[1, t], "ctx", me ^ 1)

    def wo_gets(t):
        return (hme == t) | crosses(hme, t)

    for t in range(nh):

        @pl.when((mate == t) | crosses(mate, t))
        def _():
            wo_copy(t).start()

    in_tok1.wait()
    every[me, 0, rows:] = nn(tok[rows:], w[1]).astype(BF)
    every[me, 1, rows:] = nn(tok[rows:], w[2]).astype(BF)
    in_q.wait()
    in_gain.wait()
    q_v[...] = nn(tok[...], w[0]).astype(BF)
    for i in range(3):
        in_f[i].wait()
        fb[i] = f_v[i].astype(BF)

    def gradients(s, at, slot, add, close_sum=False):
        keys = every[s, 0, :rows]
        vals = every[s, 1, :rows]
        rate = jnp.transpose(rates[at])[:, :1]
        target = (-rate * vals.astype(F32)).astype(BF)
        h1 = nn(keys, fb[0])
        h3 = nn(keys, fb[1])
        sig = jax.nn.sigmoid(h1)
        silu = h1 * sig
        act = (silu * h3).astype(BF)
        dact = nt(target, fb[2])
        d1 = (dact * h3 * (sig * (1.0 + h1 * (1.0 - sig)))).astype(BF)
        d3 = (dact * silu).astype(BF)
        new = (tn(keys, d1), tn(keys, d3), tn(act, target))
        for i in range(3):
            if close_sum:
                grad[0, i] = grad[0, i] + (grad[1, i] + new[i])
            else:
                grad[slot, i] = grad[slot, i] + new[i] if add else new[i]

    def attend(b, sources, side, gap=None, begin=False, hide=None):
        q = q_v[pl.ds(pl.multiple_of(b * rows, rows), rows)]
        span = pl.ds(side * rows, rows)
        scores = [nt(q, every[s, 0, span]) for s in sources]
        if gap is not None:
            off = (
                lax.broadcasted_iota(jnp.int32, (rows, rows), 0)
                - lax.broadcasted_iota(jnp.int32, (rows, rows), 1)
                + gap * rows
            )
            scores = [jnp.where((off >= 0) & (off < WINDOW), sc, NEG) for sc in scores]
        if hide is not None:
            scores = [sc + bias for sc, bias in zip(scores, hide)]
        top = functools.reduce(jnp.maximum, scores)
        new = jnp.max(top, axis=1, keepdims=True)
        if not begin:
            new = jnp.maximum(m_s[b], new)
        probs = [jnp.exp2((sc - new) * scale) for sc in scores]
        lane = sum(p[:, i : i + LANES] for p in probs for i in range(0, rows, LANES))
        pv = sum(nn(p.astype(BF), every[s, 1, span]) for p, s in zip(probs, sources))
        if begin:
            l_s[b] = lane
            acc[b] = pv
        else:
            fade = jnp.exp2((m_s[b] - new) * scale)
            l_s[b] = l_s[b] * fade + lane
            acc[b] = acc[b] * fade + pv
        m_s[b] = new

    def visit(c):
        sources = [me ^ c] if c == 1 else [me ^ c, me ^ c ^ 1]
        attend(jnp.where(me > me ^ c, 0, 1), sources, 0)

    def visit_before(single, chips):
        sources = [me ^ c for c in single] + [me ^ c ^ i for c in chips for i in range(2)]
        attend(1, sources, 1, hide=[jnp.where(me > s, 0.0, NEG) for s in sources])

    def visit_all(side):
        def one(s, carry):
            gap = me - s
            b = jnp.where(gap >= 0, side, 1)
            gap = gap + (b - side) * n

            @pl.when((s != me) & (gap >= 0) & (gap <= reach))
            def _():
                attend(b, [s], side, gap)

            return carry

        lax.fori_loop(0, n, one, 0)

    def fast_out(b, weights):
        q = q_v[b * rows : (b + 1) * rows]
        h1 = nn(q, weights[0])
        h3 = nn(q, weights[1])
        act = (jax.nn.silu(h1) * h3).astype(BF)
        out = nn(act, weights[2])
        inv = lax.rsqrt(jnp.mean(out * out, axis=1, keepdims=True) + norm_eps)
        normed[...] = out * inv * gain[...]

    if fine:
        gradients(me, 0, 0, False)
    fast_out(0, fb)
    attend(0, [me], 0, 0, True)
    first_hops(0)
    for turns in ((0,), later_turns):
        for kv in range(2):
            send_own(1, kv, turns)
    attend(1, [me], 1, 0, True)
    if n <= reach:
        attend(1, [me], 0, n)
    from_mate(0, 1)
    if fine:
        visit(1)
    near_hops(0)
    for c in evens:
        rate_copy(c).wait_recv()
    if fine:
        for c in evens:
            if c & (c - 1) == 0:
                gradients(me ^ c, c // 2, c // 4, c < 4)
        for c in evens:
            if c & (c - 1) == 0:
                from_mate(0, c + 1)
                visit(c)
    far_hops(0)
    if fine:
        for c in evens:
            if c & (c - 1):
                gradients(me ^ c, c // 2, 1, True, True)
    else:
        grad[0] = jnp.zeros_like(grad[0])

        def summed(j, carry):
            gradients(2 * j + core, (me // 2) ^ j, 0, True)
            return carry

        lax.fori_loop(0, n // 2, summed, 0)

    def g_copy(i):
        return remote(g_out.at[i], g_in.at[i], g_send.at[i], g_recv.at[i], "ctx", me ^ 1)

    def x_copy(i):
        return remote(g_out.at[i], g_in.at[i], x_send.at[i], x_recv.at[i], "ctx", me ^ 1)

    owned = ((0, 1), (2,))

    for own in range(2):

        @pl.when(core == own)
        def _():
            for i in owned[1 - own]:
                g_out[i] = grad[0, i].astype(BF)
                g_copy(i).start()

    chunks = comb.shape[2]
    step = rows // chunks

    def c_copy(b, u):
        return remote(
            comb.at[b, 0, u], comb.at[b, 1, u], c_send.at[b, u], c_recv.at[b, u], "head", mate
        )

    def spot(b, u):
        return pl.ds(b * rows + u * step, step)

    def p_copy(b, u, t):
        return remote(
            tok.at[spot(b, u), pl.ds(t * cols, cols)],
            part_in.at[b, hpair, u],
            p_send.at[b, u, t],
            p_recv.at[b, u, hpair],
            "head",
            t,
        )

    def combine(b):
        both = acc[b] / jnp.sum(l_s[b], axis=1, keepdims=True) + normed[...]
        for u in range(chunks):
            comb[b, 0, u] = both[u * step : (u + 1) * step].astype(BF)
            go(functools.partial(c_copy, b, u))

    def cross(b):
        for u in range(chunks):
            c_copy(b, u).wait_recv()
            for t in range(nh):

                @pl.when(crosses(hme, t))
                def _():
                    tok[spot(b, u), t * cols : (t + 1) * cols] = (
                        nn(comb[b, 0, u], wo[t]) + nn(comb[b, 1, u], wp[t])
                    ).astype(BF)
                    p_copy(b, u, t).start()

        for u in range(chunks):
            res[b, u * step : (u + 1) * step] = nn(comb[b, 0, u], wo[hme]) + nn(
                comb[b, 1, u], wp[hme]
            )

    def close(b):
        for u in range(chunks):
            for pair in range(nh // 2):

                @pl.when(hpair != pair)
                def _():
                    ref = part_in.at[b, pair, u]
                    remote(
                        ref, ref, p_send.at[b, u, 0], p_recv.at[b, u, pair], "head", mate
                    ).wait_recv()
                    here = slice(u * step, (u + 1) * step)
                    res[b, here] = res[b, here] + part_in[b, pair, u].astype(F32)

        q_v[b * rows : (b + 1) * rows] = res[b].astype(BF)
        copy = pltpu.make_async_copy(
            q_v.at[pl.ds(b * rows, rows)], mixed_h.at[b], out_sem.at[3 + b]
        )
        copy.start()
        return copy

    for t in range(nh):

        @pl.when(wo_gets(t))
        def _():
            wo_copy(t).wait_recv()
            wo_pass(t).start()

    if fine:
        for c in evens:
            if c & (c - 1):
                from_mate(0, c + 1)
                visit(c)
    else:
        for c in evens:
            from_mate(0, c + 1)
        visit_all(0)
    combine(0)

    def ns_steps(mats, count, norms=None):
        def one(_, carry):
            for at, i in enumerate(mats):
                x = grad[0, i] if norms is None else grad[0, i] * norms[at]
                xb = x.astype(BF)
                gram = nt(xb, xb)
                gb = gram.astype(BF)
                poly = coeff_b * gram + coeff_c * nn(gb, gb)
                grad[0, i] = coeff_a * x + nn(poly.astype(BF), xb)
            return carry

        if count == 1:
            one(0, 0)
        else:
            lax.fori_loop(0, count, one, 0)

    for own in range(2):

        @pl.when(core == own)
        def _():
            norms = []
            for i in owned[own]:
                g_copy(i).wait_recv()
                g = grad[0, i] + g_in[i].astype(F32)
                grad[0, i] = g
                norms.append(lax.rsqrt(jnp.sum(g * g) + norm_eps))
            ns_steps(owned[own], 1, norms)

    first_hops(1)
    for own in range(2):

        @pl.when(core == own)
        def _():
            ns_steps(owned[own], 2)

    for t in range(nh):

        @pl.when(wo_gets(t))
        def _():
            wo_pass(t).wait_recv()

    for copy in in_wo:
        copy.wait()
    cross(0)
    near_hops(1)
    for own in range(2):

        @pl.when(core == own)
        def _():
            ns_steps(owned[own], NS_STEPS - 4)

    far_hops(1)
    for own in range(2):

        @pl.when(core == own)
        def _():
            ns_steps(owned[own], 1)
            for i in owned[own]:
                g_out[i] = grad[0, i].astype(BF)
                x_copy(i).start()

    from_mate(1, 1)
    if fine:
        for far in (False, True):
            chips = [c for c in evens if far == (c & (c - 1) != 0)]
            for c in chips:
                from_mate(1, c + 1)
            visit_before([] if far else [1], chips)
    else:
        for c in evens:
            from_mate(1, c + 1)
        visit_all(1)

    def stepped(own, i):
        moved = g_out[i] if i in owned[own] else g_in[i]
        return f_v[i] - fast_step * moved.astype(F32)

    for own in range(2):

        @pl.when(core == own)
        def _():
            for i in owned[1 - own]:
                x_copy(i).wait_recv()
            for i in range(3):
                fb[i] = stepped(own, i).astype(BF)

    fast_out(1, fb)
    combine(1)
    for own in range(2):

        @pl.when(core == own)
        def _():
            for i in range(3):
                f_v[i] = stepped(own, i)

    outs = (o1_h, o3_h, o2_h)
    writes = [pltpu.make_async_copy(f_v.at[i], outs[i], out_sem.at[i]) for i in range(3)]
    for copy in writes:
        copy.start()
    writes.append(close(0))
    cross(1)
    writes.append(close(1))
    for copy in writes:
        copy.wait()
    for make in started:
        make().wait_send()
    for own in range(2):

        @pl.when(core == own)
        def _():
            for i in owned[1 - own]:
                g_copy(i).wait_send()
            for i in owned[own]:
                x_copy(i).wait_send()

    for t in range(nh):

        @pl.when((mate == t) | crosses(mate, t))
        def _():
            wo_copy(t).wait_send()

        @pl.when(wo_gets(t))
        def _():
            wo_pass(t).wait_send()

        @pl.when(crosses(hme, t))
        def _():
            for b in range(2):
                for u in range(chunks):
                    p_copy(b, u, t).wait_send()


def layer(n, nh, rows, flat, w_qkv, w_rate, f1, f3, f2, gain, wo):
    total, width = flat.shape
    blocks = total // rows
    dh, fh = f1.shape
    cols = wo.shape[1] // nh
    chunks = 4
    step = rows // chunks
    dma = pltpu.SemaphoreType.DMA
    buffers = [
        pltpu.VMEM((total, width), BF),
        pltpu.VMEM((3, width, dh), BF),
        pltpu.VMEM((1, width), BF),
        pltpu.VMEM((1, dh), F32),
        pltpu.VMEM((3, dh, fh), F32),
        pltpu.VMEM((3, dh, fh), BF),
        pltpu.VMEM((nh, dh, cols), BF),
        pltpu.VMEM((nh, dh, cols), BF),
        pltpu.VMEM((total, dh), BF),
        pltpu.VMEM((n, 2, total, dh), BF),
        pltpu.VMEM((n // 2, 8, rows), F32),
        pltpu.VMEM((2 if n <= 8 else 1, 3, dh, fh), F32),
        pltpu.VMEM((3, dh, fh), BF),
        pltpu.VMEM((3, dh, fh), BF),
        pltpu.VMEM((blocks, rows, 1), F32),
        pltpu.VMEM((blocks, rows, LANES), F32),
        pltpu.VMEM((blocks, rows, dh), F32),
        pltpu.VMEM((rows, dh), F32),
        pltpu.VMEM((blocks, 2, chunks, step, dh), BF),
        pltpu.VMEM((blocks, nh // 2, chunks, step, cols), BF),
        pltpu.VMEM((blocks, rows, cols), F32),
    ]
    need = sum(math.prod(b.shape) * jnp.dtype(b.dtype).itemsize for b in buffers)
    return pl.pallas_call(
        functools.partial(layer_kernel, n, nh, rows),
        in_specs=[HBM] * 8,
        out_specs=[ANY] * 4,
        out_shape=[jax.ShapeDtypeStruct((blocks, rows, cols), BF)]
        + [jax.ShapeDtypeStruct(f.shape, F32) for f in (f1, f3, f2)],
        scratch_shapes=[
            *buffers,
            dma((10 + nh,)),
            dma((4 * blocks, n)),
            dma((4 * blocks, n)),
            dma((n // 2,)),
            dma((n // 2,)),
            dma((3,)),
            dma((3,)),
            dma((3,)),
            dma((3,)),
            dma((2, nh)),
            dma((2, nh)),
            dma((blocks, chunks)),
            dma((blocks, chunks)),
            dma((blocks, chunks, nh)),
            dma((blocks, chunks, nh // 2)),
            dma((3 + blocks,)),
        ],
        compiler_params=pltpu.CompilerParams(
            vmem_limit_bytes=min(67_000_000, need + 6_000_000), collective_id=0, has_side_effects=True
        ),
        name="layer",
    )(
        *(
            pltpu.with_memory_space_constraint(x, pltpu.HBM)
            for x in (flat, w_qkv, w_rate, f1, f3, f2, gain, wo)
        )
    )


def shards(tokens, w_qkv, w_rate, w_out, fw_gain, fast_first, fast_third, fast_second):
    blocks, rows, width = tokens.shape
    dh = w_out.shape[1]
    mixed, *current = layer(
        lax.axis_size("ctx"),
        lax.axis_size("head"),
        rows,
        tokens.reshape(blocks * rows, width),
        w_qkv.reshape(width, 3 * dh),
        w_rate.reshape(1, width),
        fast_first[0],
        fast_third[0],
        fast_second[0],
        fw_gain,
        w_out[0],
    )
    return (mixed,) + tuple(f[None] for f in current)


def solution(mesh):
    placed = (
        P(None, "ctx", None),
        P(None, "head", None),
        P(None, "head"),
        P("head", None, None),
        P("head", None),
        P("head", None, None),
        P("head", None, None),
        P("head", None, None),
    )
    return jax.shard_map(
        shards,
        mesh=mesh,
        in_specs=placed,
        out_specs=(
            P(None, "ctx", "head"),
            P("head", None, None),
            P("head", None, None),
            P("head", None, None),
        ),
        check_vma=False,
    )
```

time: 78.6 us -> 70.3 us (0.89)
  the two profiles are of different devices: /device:TPU:10 before, /device:TPU:0 now
where the time goes in v2:
time: 70.3 us; the launch traced here: 70.2 us
  Pallas kernels  65.8 us (94%)
  local copies, waits for them, and re-layouts  3.7 us (5%)
    pallas_call x1, Pallas kernels, layer(): pl.pallas_call(functools.partial(layer_kernel, n, nh, rows), in_specs=[HB...  65.8 us
    unnamed x4, local copies, waits for them, and re-layouts  3.7 us

profile of v2, /device:TPU:0, one launch (start us, length us, event | category | flops | bytes accessed | tf_op | source)
XLA Modules:
  0.0 70.2 jit_solution(4208074256646737555)
XLA Ops:
  0.6 65.8 %layer.1 = (bf16[2,256,512]{2,1,0:T(8,128)(2,1)S(1)}, f32[512,512]{1,0:T(8,128)S(1)}, f32[512,512]{1,0:T(8,128)S(1)}, f32[512,512]{1,0:T(8,128)S(1)}) custom-call(bf16[512,2048]{1,0:T(8,128)(2,1)} %bitcast.14, bf16[2048,1536]{1,0:T(8,128)(2,1)} %bitcast.13, bf16[1,2048]{1,0:T(2,128)(2,1)} %bitcast.19, f32[512,512]{1,0:T(8,128)} %bitcast.16, ...), custom_call_target="tpu_custom_call" | custom-call | tf_op jit(solution)/shard_map/layer/pallas_call | solution.py:620
  66.5 0.8 %copy.16 = bf16[2,256,512]{2,1,0:T(8,128)(2,1)} copy(bf16[2,256,512]{2,1,0:T(8,128)(2,1)S(1)} %get-tuple-element.16) | data formatting | bytes 1048576
  67.3 1.0 %copy.17 = f32[1,512,512]{2,1,0:T(8,128)} copy(f32[1,512,512]{2,1,0:T(8,128)S(1)} %bitcast.12) | data formatting | bytes 2097152
  68.3 1.0 %copy.18 = f32[1,512,512]{2,1,0:T(8,128)} copy(f32[1,512,512]{2,1,0:T(8,128)S(1)} %bitcast.11) | data formatting | bytes 2097152
  69.2 1.0 %copy.19 = f32[1,512,512]{2,1,0:T(8,128)} copy(f32[1,512,512]{2,1,0:T(8,128)S(1)} %bitcast.10) | data formatting | bytes 2097152

commit v3 on v2

--- a/solution.py
+++ b/solution.py
@@ -47,6 +47,22 @@
     return bits if sub == 0 else bits[::-1]
 
 
+def arrivals(n):
+    slots = {}
+    for b in range(2):
+        for c in range(1, n):
+            for sub in range(2):
+                for kv in range(2):
+                    if c % 2:
+                        key = (b, c, None, None)
+                    elif c == cross_bits(n, sub)[0]:
+                        key = (b, c, sub, kv)
+                    else:
+                        key = (b, c, sub, None)
+                    slots.setdefault(key, len(slots))
+    return slots
+
+
 def remote(src, dst, send, recv, axis, peer):
     return pltpu.make_async_remote_copy(
         src_ref=src,
@@ -65,7 +81,7 @@
     tok, w, wr, gain, f_v, fb, wo, wp, q_v, every, rates,
     grad, g_out, g_in,
     m_s, l_s, acc, normed, comb, part_in, res,
-    load, k_send, k_recv, s_send, s_recv, g_send, g_recv, x_send, x_recv,
+    load, k_send, k_recv, s_send, s_recv, e_send, e_recv,
     w_send, w_recv, c_send, c_recv, p_send, p_recv, out_sem,
 ):
     me = lax.axis_index("ctx")
@@ -104,53 +120,61 @@
             device_id_type=pl.DeviceIdType.MESH,
         )
 
-    started = []
-
-    def go(make):
-        make().start()
-        started.append(make)
-
     half = rows // 2
-
-    def piece(p, c):
-        b, kv, sub = p // 4, p // 2 % 2, p % 2
-        return every.at[me ^ c, kv, pl.ds(b * rows + sub * half, half)]
-
-    def pieces(b):
-        return [(4 * b + 2 * kv + sub, sub) for kv in range(2) for sub in range(2)]
-
-    def kv_copy(p, c, bit):
-        ref = piece(p, c)
-        return remote(ref, ref, k_send.at[p, c | bit], k_recv.at[p, c | bit], "ctx", me ^ bit)
-
-    def kv_wait(p, c):
-        ref = piece(p, c)
-        remote(ref, ref, k_send.at[p, c], k_recv.at[p, c], "ctx", me ^ (c & -c)).wait_recv()
-
-    def pass_on(p, c):
-        order = cross_bits(n, p % 2)
+    slots = arrivals(n)
+
+    def piece(b, c, sub, kv):
+        span = pl.ds(b * rows, rows) if sub is None else pl.ds(b * rows + sub * half, half)
+        return every.at[me ^ c, slice(None) if kv is None else kv, span]
+
+    def slot(b, c, sub, kv):
+        for key in ((b, c, sub, kv), (b, c, sub, None), (b, c, None, None)):
+            if key in slots:
+                return slots[key]
+
+    def kv_copy(b, c, sub, kv, bit):
+        ref = piece(b, c, sub, kv)
+        return remote(
+            ref, ref, k_send.at[b, sub], k_recv.at[slot(b, c | bit, sub, kv)], "ctx", me ^ bit
+        )
+
+    def kv_wait(b, c, sub=None, kv=None):
+        ref = piece(b, c, sub, kv)
+        at = k_recv.at[slot(b, c, sub, kv)]
+        remote(ref, ref, k_send.at[0, 0], at, "ctx", me ^ (c & -c)).wait_recv()
+
+    def pass_on(b, c, sub, kv):
+        order = cross_bits(n, sub)
         last = max(i for i, bit in enumerate(order) if c & bit)
-        for bit in order[last + 1 :]:
-            go(functools.partial(kv_copy, p, c, bit))
-        go(functools.partial(kv_copy, p, c, 1))
+        for bit in order[last + 1 :] + [1]:
+            kv_copy(b, c, sub, kv, bit).start()
 
     def send_own(b, kv, turns):
         for turn in turns:
             for sub in range(2):
-                bits = cross_bits(n, sub)
-                go(functools.partial(kv_copy, 4 * b + 2 * kv + sub, 0, bits[turn]))
+                kv_copy(b, 0, sub, kv, cross_bits(n, sub)[turn]).start()
         if 0 in turns:
             for sub in range(2):
-                go(functools.partial(kv_copy, 4 * b + 2 * kv + sub, 0, 1))
+                kv_copy(b, 0, sub, kv, 1).start()
+
+    def kv_sent():
+        for b in range(2):
+            for sub in range(2):
+                ref = every.at[pl.ds(0, n - 1), :, pl.ds(0, half)]
+                remote(
+                    ref, ref, k_send.at[b, sub], k_recv.at[0], "ctx", me ^ 1
+                ).wait_send()
 
     later_turns = range(1, len(cross_bits(n, 0)))
 
     def hops(b, far, first):
         for c in evens:
-            for p, sub in pieces(b):
-                if far == (c & (c - 1) != 0) and (far or first == (c == cross_bits(n, sub)[0])):
-                    kv_wait(p, c)
-                    pass_on(p, c)
+            for kv in range(2) if first else (None,):
+                for sub in range(2):
+                    near = c == cross_bits(n, sub)[0]
+                    if far == (c & (c - 1) != 0) and (far or first == near):
+                        kv_wait(b, c, sub, kv)
+                        pass_on(b, c, sub, kv)
 
     def first_hops(b):
         hops(b, False, True)
@@ -162,38 +186,41 @@
         hops(b, True, False)
 
     def from_mate(b, c):
-        for p, _ in pieces(b):
-            kv_wait(p, c)
+        kv_wait(b, c)
 
     in_tok0.wait()
     in_k.wait()
     in_v = fetch(2, w_h.at[:, pl.ds(2 * dh, dh)], w.at[2])
-    in_wr = fetch(8 + nh, wr_h, wr)
-    in_gain = fetch(9 + nh, gain_h, gain)
+    in_wr = fetch(7, wr_h, wr)
+    in_gain = fetch(8, gain_h, gain)
     every[me, 0, :rows] = nn(tok[:rows], w[1]).astype(BF)
     pl.semaphore_wait(barrier, len(peers) + nh - 1)
     send_own(0, 0, (0,))
     in_v.wait()
     in_tok1 = fetch(3, tok_h.at[second], tok.at[second])
     in_q = fetch(4, w_h.at[:, pl.ds(0, dh)], w.at[0])
-    in_f = [fetch(5 + i, f, f_v.at[i]) for i, f in enumerate((f1_h, f3_h, f2_h))]
-    in_wo = [
-        fetch(8 + t, wo_h.at[:, pl.ds(t * cols, cols)], wo.at[t]) for t in range(nh)
-    ]
+    for i, f in enumerate((f1_h, f3_h, f2_h)):
+        fetch(5, f, f_v.at[i])
+    in_f = pltpu.make_async_copy(f_v, f_v, load.at[5])
+    for t in range(nh):
+        fetch(6, wo_h.at[:, pl.ds(t * cols, cols)], wo.at[t])
+    in_wo = pltpu.make_async_copy(wo, wo, load.at[6])
     every[me, 1, :rows] = nn(tok[:rows], w[2]).astype(BF)
     send_own(0, 1, (0,))
-    for kv in range(2):
-        send_own(0, kv, later_turns)
+    send_own(0, None, later_turns)
 
     def rate_copy(c):
         i = c // 2
-        return remote(rates.at[0], rates.at[i], s_send.at[i], s_recv.at[i], "ctx", me ^ c)
+        return remote(rates.at[0], rates.at[i], s_send, s_recv, "ctx", me ^ c)
 
     in_wr.wait()
     logit = nt(jnp.broadcast_to(wr[...], (8, wr.shape[1])), tok[:rows])
     rates[0] = jnp.maximum(logit, 0.0) + jnp.log1p(jnp.exp(-jnp.abs(logit)))
     for c in evens:
-        go(functools.partial(rate_copy, c))
+        rate_copy(c).start()
+
+    others = rates.at[pl.ds(1, n // 2 - 1)]
+    all_rates = remote(others, others, s_send, s_recv, "ctx", me ^ 1)
 
     def crosses(h, t):
         odd = lax.rem(h, 2)
@@ -232,8 +259,8 @@
     in_q.wait()
     in_gain.wait()
     q_v[...] = nn(tok[...], w[0]).astype(BF)
+    in_f.wait()
     for i in range(3):
-        in_f[i].wait()
         fb[i] = f_v[i].astype(BF)
 
     def gradients(s, at, slot, add, close_sum=False):
@@ -321,9 +348,9 @@
     fast_out(0, fb)
     attend(0, [me], 0, 0, True)
     first_hops(0)
-    for turns in ((0,), later_turns):
-        for kv in range(2):
-            send_own(1, kv, turns)
+    for kv in range(2):
+        send_own(1, kv, (0,))
+    send_own(1, None, later_turns)
     attend(1, [me], 1, 0, True)
     if n <= reach:
         attend(1, [me], 0, n)
@@ -331,8 +358,7 @@
     if fine:
         visit(1)
     near_hops(0)
-    for c in evens:
-        rate_copy(c).wait_recv()
+    all_rates.wait_recv()
     if fine:
         for c in evens:
             if c & (c - 1) == 0:
@@ -356,10 +382,10 @@
         lax.fori_loop(0, n // 2, summed, 0)
 
     def g_copy(i):
-        return remote(g_out.at[i], g_in.at[i], g_send.at[i], g_recv.at[i], "ctx", me ^ 1)
+        return remote(g_out.at[i], g_in.at[i], e_send.at[i], e_recv.at[i], "ctx", me ^ 1)
 
     def x_copy(i):
-        return remote(g_out.at[i], g_in.at[i], x_send.at[i], x_recv.at[i], "ctx", me ^ 1)
+        return remote(g_out.at[i], g_in.at[i], e_send.at[i], e_recv.at[i], "ctx", me ^ 1)
 
     owned = ((0, 1), (2,))
 
@@ -372,11 +398,12 @@
                 g_copy(i).start()
 
     chunks = comb.shape[2]
+    pairs = nh // 2
     step = rows // chunks
 
     def c_copy(b, u):
         return remote(
-            comb.at[b, 0, u], comb.at[b, 1, u], c_send.at[b, u], c_recv.at[b, u], "head", mate
+            comb.at[b, 0, u], comb.at[b, 1, u], c_send.at[b], c_recv.at[b, u], "head", mate
         )
 
     def spot(b, u):
@@ -385,9 +412,9 @@
     def p_copy(b, u, t):
         return remote(
             tok.at[spot(b, u), pl.ds(t * cols, cols)],
-            part_in.at[b, hpair, u],
-            p_send.at[b, u, t],
-            p_recv.at[b, u, hpair],
+            part_in.at[b, lax.rem(hpair - t // 2 + pairs, pairs) - 1, u],
+            p_send.at[b, t],
+            p_recv.at[b, u, lax.rem(hpair - t // 2 + pairs, pairs) - 1],
             "head",
             t,
         )
@@ -396,7 +423,7 @@
         both = acc[b] / jnp.sum(l_s[b], axis=1, keepdims=True) + normed[...]
         for u in range(chunks):
             comb[b, 0, u] = both[u * step : (u + 1) * step].astype(BF)
-            go(functools.partial(c_copy, b, u))
+            c_copy(b, u).start()
 
     def cross(b):
         for u in range(chunks):
@@ -417,20 +444,15 @@
 
     def close(b):
         for u in range(chunks):
-            for pair in range(nh // 2):
-
-                @pl.when(hpair != pair)
-                def _():
-                    ref = part_in.at[b, pair, u]
-                    remote(
-                        ref, ref, p_send.at[b, u, 0], p_recv.at[b, u, pair], "head", mate
-                    ).wait_recv()
-                    here = slice(u * step, (u + 1) * step)
-                    res[b, here] = res[b, here] + part_in[b, pair, u].astype(F32)
+            for pair in range(pairs - 1):
+                ref = part_in.at[b, pair, u]
+                remote(ref, ref, p_send.at[b, 0], p_recv.at[b, u, pair], "head", mate).wait_recv()
+                here = slice(u * step, (u + 1) * step)
+                res[b, here] = res[b, here] + part_in[b, pair, u].astype(F32)
 
         q_v[b * rows : (b + 1) * rows] = res[b].astype(BF)
         copy = pltpu.make_async_copy(
-            q_v.at[pl.ds(b * rows, rows)], mixed_h.at[b], out_sem.at[3 + b]
+            q_v.at[pl.ds(b * rows, rows)], mixed_h.at[b], out_sem.at[1 + b]
         )
         copy.start()
         return copy
@@ -494,8 +516,7 @@
         def _():
             wo_pass(t).wait_recv()
 
-    for copy in in_wo:
-        copy.wait()
+    in_wo.wait()
     cross(0)
     near_hops(1)
     for own in range(2):
@@ -549,16 +570,20 @@
                 f_v[i] = stepped(own, i)
 
     outs = (o1_h, o3_h, o2_h)
-    writes = [pltpu.make_async_copy(f_v.at[i], outs[i], out_sem.at[i]) for i in range(3)]
+    writes = [pltpu.make_async_copy(f_v.at[i], outs[i], out_sem.at[0]) for i in range(3)]
     for copy in writes:
         copy.start()
+    writes = [pltpu.make_async_copy(f_v, f_v, out_sem.at[0])]
     writes.append(close(0))
     cross(1)
     writes.append(close(1))
     for copy in writes:
         copy.wait()
-    for make in started:
-        make().wait_send()
+    kv_sent()
+    all_rates.wait_send()
+    for b in range(2):
+        ref = comb.at[b, 0]
+        remote(ref, ref, c_send.at[b], c_recv.at[b, 0], "head", mate).wait_send()
     for own in range(2):
 
         @pl.when(core == own)
@@ -581,8 +606,8 @@
         @pl.when(crosses(hme, t))
         def _():
             for b in range(2):
-                for u in range(chunks):
-                    p_copy(b, u, t).wait_send()
+                ref = tok.at[pl.ds(b * rows, rows), pl.ds(t * cols, cols)]
+                remote(ref, ref, p_send.at[b, t], p_recv.at[0, 0, 0], "head", mate).wait_send()
 
 
 def layer(n, nh, rows, flat, w_qkv, w_rate, f1, f3, f2, gain, wo):
@@ -613,7 +638,7 @@
         pltpu.VMEM((blocks, rows, dh), F32),
         pltpu.VMEM((rows, dh), F32),
         pltpu.VMEM((blocks, 2, chunks, step, dh), BF),
-        pltpu.VMEM((blocks, nh // 2, chunks, step, cols), BF),
+        pltpu.VMEM((blocks, nh // 2 - 1, chunks, step, cols), BF),
         pltpu.VMEM((blocks, rows, cols), F32),
     ]
     need = sum(math.prod(b.shape) * jnp.dtype(b.dtype).itemsize for b in buffers)
@@ -625,22 +650,20 @@
         + [jax.ShapeDtypeStruct(f.shape, F32) for f in (f1, f3, f2)],
         scratch_shapes=[
             *buffers,
-            dma((10 + nh,)),
-            dma((4 * blocks, n)),
-            dma((4 * blocks, n)),
-            dma((n // 2,)),
-            dma((n // 2,)),
-            dma((3,)),
-            dma((3,)),
+            dma((9,)),
+            dma((blocks, 2)),
+            dma((len(arrivals(n)),)),
+            dma,
+            dma,
             dma((3,)),
             dma((3,)),
             dma((2, nh)),
             dma((2, nh)),
+            dma((blocks,)),
             dma((blocks, chunks)),
-            dma((blocks, chunks)),
-            dma((blocks, chunks, nh)),
-            dma((blocks, chunks, nh // 2)),
-            dma((3 + blocks,)),
+            dma((blocks, nh)),
+            dma((blocks, chunks, nh // 2 - 1)),
+            dma((1 + blocks,)),
         ],
         compiler_params=pltpu.CompilerParams(
             vmem_limit_bytes=min(67_000_000, need + 6_000_000), collective_id=0, has_side_effects=True
@@ -654,10 +677,34 @@
     )
 
 
+def write_kernel(*refs):
+    half = len(refs) // 2
+    sems = refs[-1]
+    copies = [
+        pltpu.make_async_copy(refs[i], refs[half + i], sems.at[i]) for i in range(half)
+    ]
+    for copy in copies:
+        copy.start()
+    for copy in copies:
+        copy.wait()
+
+
+def write_out(arrays):
+    return pl.pallas_call(
+        write_kernel,
+        in_specs=[ANY] * len(arrays),
+        out_specs=[HBM] * len(arrays),
+        out_shape=[jax.ShapeDtypeStruct(a.shape, a.dtype) for a in arrays],
+        scratch_shapes=[pltpu.SemaphoreType.DMA((len(arrays),))],
+        compiler_params=pltpu.CompilerParams(vmem_limit_bytes=4_000_000),
+        name="write_out",
+    )(*arrays)
+
+
 def shards(tokens, w_qkv, w_rate, w_out, fw_gain, fast_first, fast_third, fast_second):
     blocks, rows, width = tokens.shape
     dh = w_out.shape[1]
-    mixed, *current = layer(
+    done = layer(
         lax.axis_size("ctx"),
         lax.axis_size("head"),
         rows,
@@ -670,6 +717,7 @@
         fw_gain,
         w_out[0],
     )
+    mixed, *current = write_out(done)
     return (mixed,) + tuple(f[None] for f in current)
 
 

time: 70.3 us -> 67.2 us (0.956)
  local copies, waits for them, and re-layouts: 3.7 us -> 0 us
    unnamed x4 -> x0, local copies, waits for them, and re-layouts: 3.7 us -> none
    pallas_call x0 -> x1, Pallas kernels: none -> 1.87 us  [write_out(): pl.pallas_call(write_kernel, in_specs=[ANY] * len(arrays), out_specs=[HBM...]
    pallas_call x1, Pallas kernels: 65.8 us -> 64.4 us  [layer(): pl.pallas_call(functools.partial(layer_kernel, n, nh, rows), in_specs=[HB...]
where the time goes in v3:
time: 67.2 us; the launch traced here: 67.1 us
  Pallas kernels  66.2 us (99%)
  between operations  0.82 us (1%)
    pallas_call x1, Pallas kernels, layer(): pl.pallas_call(functools.partial(layer_kernel, n, nh, rows), in_specs=[HB...  64.4 us
    pallas_call x1, Pallas kernels, write_out(): pl.pallas_call(write_kernel, in_specs=[ANY] * len(arrays), out_specs=[HBM...  1.87 us

profile of v3, /device:TPU:0, one launch (start us, length us, event | category | flops | bytes accessed | tf_op | source)
XLA Modules:
  0.0 67.1 jit_solution(2853100510762453758)
XLA Ops:
  0.6 64.4 %layer.1 = (bf16[2,256,512]{2,1,0:T(8,128)(2,1)S(1)}, f32[512,512]{1,0:T(8,128)S(1)}, f32[512,512]{1,0:T(8,128)S(1)}, f32[512,512]{1,0:T(8,128)S(1)}) custom-call(bf16[512,2048]{1,0:T(8,128)(2,1)} %bitcast.11, bf16[2048,1536]{1,0:T(8,128)(2,1)} %bitcast.10, bf16[1,2048]{1,0:T(2,128)(2,1)} %bitcast.16, f32[512,512]{1,0:T(8,128)} %bitcast.13, ...), custom_call_target="tpu_custom_call" | custom-call | tf_op jit(solution)/shard_map/layer/pallas_call | solution.py:645
  65.0 1.9 %write_out.1 = (bf16[2,256,512]{2,1,0:T(8,128)(2,1)}, f32[512,512]{1,0:T(8,128)}, f32[512,512]{1,0:T(8,128)}, f32[512,512]{1,0:T(8,128)}) custom-call(bf16[2,256,512]{2,1,0:T(8,128)(2,1)S(1)} %get-tuple-element.12.refs_0_, f32[512,512]{1,0:T(8,128)S(1)} %get-tuple-element.13.refs_1_, f32[512,512]{1,0:T(8,128)S(1)} %get-tuple-element.14.refs_2_, ...), custom_call_target="tpu_custom_call" | custom-call | tf_op jit(solution)/shard_map/write_out/pallas_call | solution.py:693

commit v4 on v3

--- a/solution.py
+++ b/solution.py
@@ -425,22 +425,40 @@
             comb[b, 0, u] = both[u * step : (u + 1) * step].astype(BF)
             c_copy(b, u).start()
 
+    targets = sorted(range(nh), key=lambda t: -abs(2 * t - nh + 1))
+
     def cross(b):
-        for u in range(chunks):
-            c_copy(b, u).wait_recv()
-            for t in range(nh):
-
-                @pl.when(crosses(hme, t))
-                def _():
-                    tok[spot(b, u), t * cols : (t + 1) * cols] = (
-                        nn(comb[b, 0, u], wo[t]) + nn(comb[b, 1, u], wp[t])
+        if b == 0:
+            for u in range(chunks):
+                c_copy(b, u).wait_recv()
+        for t in targets:
+
+            @pl.when(crosses(hme, t))
+            def _():
+                if b == 0:
+                    mine, pair = (comb[b, k].reshape(rows, dh) for k in range(2))
+                    tok[b * rows : (b + 1) * rows, t * cols : (t + 1) * cols] = (
+                        nn(mine, wo[t]) + nn(pair, wp[t])
                     ).astype(BF)
+                for u in range(chunks):
+                    if b > 0:
+                        if t == 0 or t == nh - 1:
+                            c_copy(b, u).wait_recv()
+                        tok[spot(b, u), t * cols : (t + 1) * cols] = (
+                            nn(comb[b, 0, u], wo[t]) + nn(comb[b, 1, u], wp[t])
+                        ).astype(BF)
                     p_copy(b, u, t).start()
 
-        for u in range(chunks):
-            res[b, u * step : (u + 1) * step] = nn(comb[b, 0, u], wo[hme]) + nn(
-                comb[b, 1, u], wp[hme]
-            )
+    def own_part(b):
+        if b > 0:
+
+            @pl.when(jnp.logical_not(crosses(hme, 0) | crosses(hme, nh - 1)))
+            def _():
+                for u in range(chunks):
+                    c_copy(b, u).wait_recv()
+
+        mine, pair = (comb[b, k].reshape(rows, dh) for k in range(2))
+        res[b] = nn(mine, wo[hme]) + nn(pair, wp[hme])
 
     def close(b):
         for u in range(chunks):
@@ -518,14 +536,13 @@
 
     in_wo.wait()
     cross(0)
+    for own in range(2):
+
+        @pl.when(core == own)
+        def _():
+            ns_steps(owned[own], NS_STEPS - 4)
+
     near_hops(1)
-    for own in range(2):
-
-        @pl.when(core == own)
-        def _():
-            ns_steps(owned[own], NS_STEPS - 4)
-
-    far_hops(1)
     for own in range(2):
 
         @pl.when(core == own)
@@ -535,32 +552,37 @@
                 g_out[i] = grad[0, i].astype(BF)
                 x_copy(i).start()
 
+    def second(far):
+        chips = [c for c in evens if far == (c & (c - 1) != 0)]
+        for c in chips:
+            from_mate(1, c + 1)
+        visit_before([] if far else [1], chips)
+
     from_mate(1, 1)
     if fine:
-        for far in (False, True):
-            chips = [c for c in evens if far == (c & (c - 1) != 0)]
-            for c in chips:
-                from_mate(1, c + 1)
-            visit_before([] if far else [1], chips)
+        second(False)
+    far_hops(1)
+
+    def stepped(own, i):
+        moved = g_out[i] if i in owned[own] else g_in[i]
+        return f_v[i] - fast_step * moved.astype(F32)
+
+    for own in range(2):
+
+        @pl.when(core == own)
+        def _():
+            for i in owned[1 - own]:
+                x_copy(i).wait_recv()
+            for i in range(3):
+                fb[i] = stepped(own, i).astype(BF)
+
+    fast_out(1, fb)
+    if fine:
+        second(True)
     else:
         for c in evens:
             from_mate(1, c + 1)
         visit_all(1)
-
-    def stepped(own, i):
-        moved = g_out[i] if i in owned[own] else g_in[i]
-        return f_v[i] - fast_step * moved.astype(F32)
-
-    for own in range(2):
-
-        @pl.when(core == own)
-        def _():
-            for i in owned[1 - own]:
-                x_copy(i).wait_recv()
-            for i in range(3):
-                fb[i] = stepped(own, i).astype(BF)
-
-    fast_out(1, fb)
     combine(1)
     for own in range(2):
 
@@ -574,8 +596,10 @@
     for copy in writes:
         copy.start()
     writes = [pltpu.make_async_copy(f_v, f_v, out_sem.at[0])]
+    own_part(0)
+    cross(1)
+    own_part(1)
     writes.append(close(0))
-    cross(1)
     writes.append(close(1))
     for copy in writes:
         copy.wait()

time: 67.2 us -> 63.2 us (0.940)
  the two profiles are of different devices: /device:TPU:0 before, /device:TPU:10 now
where the time goes in v4:
time: 63.2 us; the launch traced here: 63.1 us
  Pallas kernels  62.2 us (98%)
  between operations  0.82 us (1%)
    pallas_call x1, Pallas kernels, layer(): pl.pallas_call(functools.partial(layer_kernel, n, nh, rows), in_specs=[HB...  60.4 us
    pallas_call x1, Pallas kernels, write_out(): pl.pallas_call(write_kernel, in_specs=[ANY] * len(arrays), out_specs=[HBM...  1.87 us

profile of v4, /device:TPU:10, one launch (start us, length us, event | category | flops | bytes accessed | tf_op | source)
XLA Modules:
  0.0 63.1 jit_solution(8410572680398206262)
XLA Ops:
  0.6 60.4 %layer.1 = (bf16[2,256,512]{2,1,0:T(8,128)(2,1)S(1)}, f32[512,512]{1,0:T(8,128)S(1)}, f32[512,512]{1,0:T(8,128)S(1)}, f32[512,512]{1,0:T(8,128)S(1)}) custom-call(bf16[512,2048]{1,0:T(8,128)(2,1)} %bitcast.11, bf16[2048,1536]{1,0:T(8,128)(2,1)} %bitcast.10, bf16[1,2048]{1,0:T(2,128)(2,1)} %bitcast.16, f32[512,512]{1,0:T(8,128)} %bitcast.13, ...), custom_call_target="tpu_custom_call" | custom-call | tf_op jit(solution)/shard_map/layer/pallas_call | solution.py:669
  61.0 1.9 %write_out.1 = (bf16[2,256,512]{2,1,0:T(8,128)(2,1)}, f32[512,512]{1,0:T(8,128)}, f32[512,512]{1,0:T(8,128)}, f32[512,512]{1,0:T(8,128)}) custom-call(bf16[2,256,512]{2,1,0:T(8,128)(2,1)S(1)} %get-tuple-element.12.refs_0_, f32[512,512]{1,0:T(8,128)S(1)} %get-tuple-element.13.refs_1_, f32[512,512]{1,0:T(8,128)S(1)} %get-tuple-element.14.refs_2_, ...), custom_call_target="tpu_custom_call" | custom-call | tf_op jit(solution)/shard_map/write_out/pallas_call | solution.py:717

commit v5 on v4

--- a/solution.py
+++ b/solution.py
@@ -103,8 +103,14 @@
         return copy
 
     first, second = pl.ds(0, rows), pl.ds(rows, rows)
-    in_tok0 = fetch(0, tok_h.at[first], tok.at[first])
-    in_k = fetch(1, w_h.at[:, pl.ds(dh, dh)], w.at[1])
+    def fetch_rows(i, src, dst, parts):
+        size = dst.shape[0] // parts
+        for at in range(0, dst.shape[0], size):
+            fetch(i, src.at[pl.ds(at, size)], dst.at[pl.ds(at, size)])
+        return pltpu.make_async_copy(dst, dst, load.at[i])
+
+    in_tok0 = fetch_rows(0, tok_h.at[first], tok.at[first], 2)
+    in_k = fetch_rows(1, w_h.at[:, pl.ds(dh, dh)], w.at[1], 4)
 
     barrier = pltpu.get_barrier_semaphore()
     peers = [1] + evens
@@ -190,7 +196,7 @@
 
     in_tok0.wait()
     in_k.wait()
-    in_v = fetch(2, w_h.at[:, pl.ds(2 * dh, dh)], w.at[2])
+    in_v = fetch_rows(2, w_h.at[:, pl.ds(2 * dh, dh)], w.at[2], 4)
     in_wr = fetch(7, wr_h, wr)
     in_gain = fetch(8, gain_h, gain)
     every[me, 0, :rows] = nn(tok[:rows], w[1]).astype(BF)
@@ -493,41 +499,55 @@
         visit_all(0)
     combine(0)
 
-    def ns_steps(mats, count, norms=None):
+    def ns_step(i, norm=None):
+        x = grad[0, i]
+        xb = x.astype(BF)
+        gram = nt(xb, xb)
+        if norm is not None:
+            gram = gram * (norm * norm)
+        gb = gram.astype(BF)
+        poly = coeff_b * gram + coeff_c * nn(gb, gb)
+        new = coeff_a * x + nn(poly.astype(BF), xb)
+        grad[0, i] = new if norm is None else new * norm
+
+    def ns_steps(mats, count):
         def one(_, carry):
-            for at, i in enumerate(mats):
-                x = grad[0, i] if norms is None else grad[0, i] * norms[at]
-                xb = x.astype(BF)
-                gram = nt(xb, xb)
-                gb = gram.astype(BF)
-                poly = coeff_b * gram + coeff_c * nn(gb, gb)
-                grad[0, i] = coeff_a * x + nn(poly.astype(BF), xb)
+            for i in mats:
+                ns_step(i)
             return carry
 
-        if count == 1:
-            one(0, 0)
-        else:
-            lax.fori_loop(0, count, one, 0)
+        lax.fori_loop(0, count, one, 0)
 
     for own in range(2):
 
         @pl.when(core == own)
         def _():
+            for i in owned[own]:
+                g_copy(i).wait_recv()
             norms = []
             for i in owned[own]:
-                g_copy(i).wait_recv()
                 g = grad[0, i] + g_in[i].astype(F32)
                 grad[0, i] = g
                 norms.append(lax.rsqrt(jnp.sum(g * g) + norm_eps))
-            ns_steps(owned[own], 1, norms)
-
-    first_hops(1)
+            for i, norm in zip(owned[own], norms):
+                ns_step(i, norm)
+
+    for count in range(2):
+        if count == 1:
+            first_hops(1)
+        for own in range(2):
+
+            @pl.when(core == own)
+            def _():
+                ns_steps(owned[own], 1)
+
     for own in range(2):
 
         @pl.when(core == own)
         def _():
-            ns_steps(owned[own], 2)
-
+            ns_steps(owned[own], NS_STEPS - 4)
+
+    near_hops(1)
     for t in range(nh):
 
         @pl.when(wo_gets(t))
@@ -540,15 +560,8 @@
 
         @pl.when(core == own)
         def _():
-            ns_steps(owned[own], NS_STEPS - 4)
-
-    near_hops(1)
-    for own in range(2):
-
-        @pl.when(core == own)
-        def _():
-            ns_steps(owned[own], 1)
             for i in owned[own]:
+                ns_step(i)
                 g_out[i] = grad[0, i].astype(BF)
                 x_copy(i).start()
 
@@ -559,6 +572,7 @@
         visit_before([] if far else [1], chips)
 
     from_mate(1, 1)
+
     if fine:
         second(False)
     far_hops(1)
@@ -576,14 +590,16 @@
             for i in range(3):
                 fb[i] = stepped(own, i).astype(BF)
 
-    fast_out(1, fb)
     if fine:
+        fast_out(1, fb)
         second(True)
+        combine(1)
     else:
+        fast_out(1, fb)
         for c in evens:
             from_mate(1, c + 1)
         visit_all(1)
-    combine(1)
+        combine(1)
     for own in range(2):
 
         @pl.when(core == own)

time: 63.2 us -> 63.1 us (level)
  no operation moved by 1% of the time
where the time goes in v5:
time: 63.1 us; the launch traced here: 63 us
  Pallas kernels  62.2 us (99%)
  between operations  0.82 us (1%)
    pallas_call x1, Pallas kernels, layer(): pl.pallas_call(functools.partial(layer_kernel, n, nh, rows), in_specs=[HB...  60.3 us
    pallas_call x1, Pallas kernels, write_out(): pl.pallas_call(write_kernel, in_specs=[ANY] * len(arrays), out_specs=[HBM...  1.87 us

profile of v5, /device:TPU:10, one launch (start us, length us, event | category | flops | bytes accessed | tf_op | source)
XLA Modules:
  0.0 63.0 jit_solution(5392506185093572459)
XLA Ops:
  0.6 60.3 %layer.1 = (bf16[2,256,512]{2,1,0:T(8,128)(2,1)S(1)}, f32[512,512]{1,0:T(8,128)S(1)}, f32[512,512]{1,0:T(8,128)S(1)}, f32[512,512]{1,0:T(8,128)S(1)}) custom-call(bf16[512,2048]{1,0:T(8,128)(2,1)} %bitcast.11, bf16[2048,1536]{1,0:T(8,128)(2,1)} %bitcast.10, bf16[1,2048]{1,0:T(2,128)(2,1)} %bitcast.16, f32[512,512]{1,0:T(8,128)} %bitcast.13, ...), custom_call_target="tpu_custom_call" | custom-call | tf_op jit(solution)/shard_map/layer/pallas_call | solution.py:685
  60.9 1.9 %write_out.1 = (bf16[2,256,512]{2,1,0:T(8,128)(2,1)}, f32[512,512]{1,0:T(8,128)}, f32[512,512]{1,0:T(8,128)}, f32[512,512]{1,0:T(8,128)}) custom-call(bf16[2,256,512]{2,1,0:T(8,128)(2,1)S(1)} %get-tuple-element.12.refs_0_, f32[512,512]{1,0:T(8,128)S(1)} %get-tuple-element.13.refs_1_, f32[512,512]{1,0:T(8,128)S(1)} %get-tuple-element.14.refs_2_, ...), custom_call_target="tpu_custom_call" | custom-call | tf_op jit(solution)/shard_map/write_out/pallas_call | solution.py:733

commit v6 on v5

--- a/solution.py
+++ b/solution.py
@@ -720,13 +720,13 @@
 def write_kernel(*refs):
     half = len(refs) // 2
     sems = refs[-1]
-    copies = [
-        pltpu.make_async_copy(refs[i], refs[half + i], sems.at[i]) for i in range(half)
-    ]
-    for copy in copies:
-        copy.start()
-    for copy in copies:
-        copy.wait()
+    for i in range(half):
+        size = refs[i].shape[-2] // 2
+        for at in range(2):
+            span = (slice(None),) * (len(refs[i].shape) - 2) + (pl.ds(at * size, size),)
+            pltpu.make_async_copy(refs[i].at[span], refs[half + i].at[span], sems.at[i]).start()
+    for i in range(half):
+        pltpu.make_async_copy(refs[i], refs[half + i], sems.at[i]).wait()
 
 
 def write_out(arrays):

time: 63.1 us -> 63.1 us (level)
  no operation moved by 1% of the time
where the time goes in v6:
time: 63.1 us; the launch traced here: 63 us
  Pallas kernels  62.2 us (99%)
  between operations  0.82 us (1%)
    pallas_call x1, Pallas kernels, layer(): pl.pallas_call(functools.partial(layer_kernel, n, nh, rows), in_specs=[HB...  60.3 us
    pallas_call x1, Pallas kernels, write_out(): pl.pallas_call(write_kernel, in_specs=[ANY] * len(arrays), out_specs=[HBM...  1.87 us

profile of v6, /device:TPU:10, one launch (start us, length us, event | category | flops | bytes accessed | tf_op | source)
XLA Modules:
  0.0 63.0 jit_solution(4019174418375724268)
XLA Ops:
  0.6 60.3 %layer.1 = (bf16[2,256,512]{2,1,0:T(8,128)(2,1)S(1)}, f32[512,512]{1,0:T(8,128)S(1)}, f32[512,512]{1,0:T(8,128)S(1)}, f32[512,512]{1,0:T(8,128)S(1)}) custom-call(bf16[512,2048]{1,0:T(8,128)(2,1)} %bitcast.11, bf16[2048,1536]{1,0:T(8,128)(2,1)} %bitcast.10, bf16[1,2048]{1,0:T(2,128)(2,1)} %bitcast.16, f32[512,512]{1,0:T(8,128)} %bitcast.13, ...), custom_call_target="tpu_custom_call" | custom-call | tf_op jit(solution)/shard_map/layer/pallas_call | solution.py:685
  60.9 1.9 %write_out.1 = (bf16[2,256,512]{2,1,0:T(8,128)(2,1)}, f32[512,512]{1,0:T(8,128)}, f32[512,512]{1,0:T(8,128)}, f32[512,512]{1,0:T(8,128)}) custom-call(bf16[2,256,512]{2,1,0:T(8,128)(2,1)S(1)} %get-tuple-element.12.refs_0_, f32[512,512]{1,0:T(8,128)S(1)} %get-tuple-element.13.refs_1_, f32[512,512]{1,0:T(8,128)S(1)} %get-tuple-element.14.refs_2_, ...), custom_call_target="tpu_custom_call" | custom-call | tf_op jit(solution)/shard_map/write_out/pallas_call | solution.py:733
